TPU v7x, 256 devices: a whole 4x4x8 slice. The times are simulated.
256 devices in a mesh: dp: 16 (over y_hi, x, core), mp: 16 (over z, y_lo).
Axes of the slice: x: 4, y: 4 (y_hi: 2, y_lo: 2; y = y_hi * 2 + y_lo), z: 8, core: 2. Of those that a mesh axis runs over, the one named last changes fastest.
Arguments:
- tokens: bfloat16 [8192, 8192], P(('dp', 'mp')), parts along dimension 0, may hold values from -6 to 6
- norm_gain: float32 [8192], replicated, may hold values from 0.5 to 1.5
- qkv_weight: bfloat16 [8192, 10240], P(None, 'mp'), may hold values from -0.0625 to 0.0625
- qkv_bias: float32 [10240], P('mp'), may hold values from -3 to 3
- qkv_grad: bfloat16 [8192, 10240], P('dp', 'mp'), parts along dimension 0, may hold values from -6 to 6
Outputs:
- qkv: bfloat16 [8192, 10240], P('dp', 'mp'), parts along dimension 0
- tokens_grad: float32 [8192, 8192], P(('dp', 'mp')), parts along dimension 0
- gain_grad: float32 [131072], P('dp'), parts along dimension 0
- bias_grad: float32 [163840], P(('dp', 'mp')), parts along dimension 0
There are 16 independent parts, one for each index of `dp`. A program takes and returns all parts, laid end to end along the dimension named above; an argument that names none is the same for every part. Nothing has to cross between parts.
All inputs are finite; a program needn't handle non-finite values.
Results may differ from a plain program's by a relative error of at most 0.0046.
Values may be sent and summed in bfloat16 or wider, within the bound.
A program may use at most 128 MiB of HBM per device.

v0:
```python
import functools

import jax
import jax.numpy as jnp
import numpy as np
from jax import lax
from jax.experimental import pallas as pl
from jax.experimental.pallas import tpu as pltpu
from jax.sharding import PartitionSpec as P

HEAD_DIM = 128
SEQ_LEN = 32768
GROUP = 10
CHUNKS = 4
TILE_K = 512
MESH = pl.DeviceIdType.MESH


def rope_tables(rows, tok_dev, stride):
    half = HEAD_DIM // 2
    row = np.arange(rows)
    place = (row // tok_dev * stride + row % tok_dev).astype(np.float32)
    inverse = np.exp(
        -np.log(np.float32(1000000.0))
        * (np.float32(2.0) * np.arange(half).astype(np.float32) / np.float32(HEAD_DIM))
    ).astype(np.float32)
    angle = (place[:, None] * inverse[None, :]).astype(np.float32)
    cosine, sine = np.cos(angle).astype(np.float32), np.sin(angle).astype(np.float32)
    return np.concatenate([cosine, cosine], 1), np.concatenate([-sine, sine], 1)


def kernel(
    n,
    tok_h, gain_h, w_h, bias_h, grad_h, cos_h, sin_h,
    qkv, tg, gg_ref, bg_ref,
    tok, gain, w, bias, grad, cos, sin,
    low, part, held, run, acc, ng, scale_ref, gmine, gsend, grecv,
    in_sem, w_sem, send_sem, recv_sem, gsend_sem, grecv_sem,
):
    me = lax.axis_index("mp")
    rows, depth = tok.shape
    width = w.shape[1]
    heads = width // HEAD_DIM
    span = depth // CHUNKS
    tiles = depth // TILE_K
    per = tiles // CHUNKS
    f32 = jnp.float32

    has_right, has_left = me < n - 1, me > 0
    barrier = pltpu.get_barrier_semaphore()
    for there, k in ((has_right, 1), (has_left, n - 1)):
        @pl.when(there)
        def _():
            pl.semaphore_signal(
                barrier, inc=1, device_id={"mp": lax.rem(me + k, n)}, device_id_type=MESH
            )

    loads = []
    for i, (src, dst) in enumerate(
        ((tok_h, tok), (gain_h, gain.at[0]), (grad_h, grad), (cos_h, cos), (sin_h, sin), (bias_h, bias.at[0]))
    ):
        c = pltpu.make_async_copy(src, dst, in_sem.at[i])
        c.start()
        loads.append(c)

    def w_copy(i):
        k = pl.ds(pl.multiple_of(i * TILE_K, TILE_K), TILE_K)
        return pltpu.make_async_copy(w_h.at[k, :], w.at[k, :], w_sem.at[i])

    def block(s):
        return pl.ds(pl.multiple_of(s * rows, rows), rows)

    def cols(c):
        return pl.ds(pl.multiple_of(c * span, span), span)

    loads[0].wait()
    loads[1].wait()
    total = jnp.zeros((rows, 1), f32)
    for c in range(CHUNKS):
        v = tok[:, c * span:(c + 1) * span].astype(f32)
        total = total + jnp.sum(v * v, axis=1, keepdims=True)
    scale = lax.rsqrt(total / depth + 1e-06)
    scale_ref[...] = jnp.broadcast_to(scale, scale_ref.shape)
    for c in range(CHUNKS):
        ks = slice(c * span, (c + 1) * span)
        held[block(me), ks] = (tok[:, ks].astype(f32) * scale * gain[:, ks]).astype(jnp.bfloat16)
    inside = has_right & has_left

    @pl.when(inside)
    def _():
        pl.semaphore_wait(barrier, 2)

    @pl.when(jnp.logical_not(inside))
    def _():
        pl.semaphore_wait(barrier, 1)


    def transfer(way, buf, at, j, c):
        ref = buf.at[block(at), cols(c)]
        return pltpu.make_async_remote_copy(
            src_ref=ref,
            dst_ref=ref,
            send_sem=send_sem.at[way, j, c],
            recv_sem=recv_sem.at[way, j, c],
            device_id={"mp": lax.rem(me + (1 if way == 0 else n - 1), n)},
            device_id_type=MESH,
        )

    def step(j, c):
        for way, goes, comes, back in ((0, has_right, has_left, me), (1, has_left, has_right, n - 1 - me)):
            @pl.when(comes)
            def _():
                transfer(way, held, 0, j - 1, c).wait_recv()

            @pl.when(goes)
            def _():
                @pl.when(j <= back)
                def _():
                    transfer(way, held, me - j if way == 0 else me + j, j, c).start()

                @pl.when(j > back)
                def _():
                    t = n - j + me if way == 0 else j - n + me
                    slot = t + 1 if way == 0 else t

                    @pl.when(comes)
                    def _():
                        value = part[block(t), cols(c)] + run[block(slot), cols(c)].astype(f32)
                        run[block(slot), cols(c)] = value.astype(jnp.bfloat16)

                    @pl.when(jnp.logical_not(comes))
                    def _():
                        run[block(slot), cols(c)] = part[block(t), cols(c)].astype(jnp.bfloat16)

                    transfer(way, run, slot, j, c).start()

    for c in range(CHUNKS):
        for way, goes in ((0, has_right), (1, has_left)):
            @pl.when(goes)
            def _():
                transfer(way, held, me, 0, c).start()

    @pl.loop(0, tiles)
    def _(i):
        w_copy(i).start()

    for l in loads[2:]:
        l.wait()
    for h in range(heads):
        hs = slice(h * HEAD_DIM, (h + 1) * HEAD_DIM)
        x = grad[:, hs].astype(f32)
        turned = x * cos[...] - pltpu.roll(x, HEAD_DIM // 2, 1) * sin[...]
        plain = lax.rem(me * heads + h, GROUP) == GROUP - 1
        x = jnp.where(plain, x, turned)
        bg_ref[:, hs] = jnp.sum(x, axis=0, keepdims=True)
        low[:, hs] = x.astype(jnp.bfloat16)

    def backward(c):
        @pl.loop(0, per)
        def _(i):
            at = c * per + i
            w_copy(at).wait()
            k = pl.ds(pl.multiple_of(at * TILE_K, TILE_K), TILE_K)
            part[:, k] = lax.dot_general(
                low[...], w[k, :], (((1,), (1,)), ((), ())), preferred_element_type=f32
            )

    @pl.loop(0, CHUNKS)
    def _(c):
        backward(c)

        @pl.when(c > 0)
        def _():
            step(1, c - 1)

    step(1, CHUNKS - 1)

    @pl.loop(2, n - 1)
    def _(j):
        @pl.loop(0, CHUNKS)
        def _(c):
            step(j, c)

    tile_n = 640 if width % 640 == 0 else HEAD_DIM
    tiles_n = width // tile_n

    def gain_copy(k, c):
        return pltpu.make_async_remote_copy(
            src_ref=gsend.at[c],
            dst_ref=grecv.at[k - 1, c],
            send_sem=gsend_sem.at[k - 1, c],
            recv_sem=grecv_sem.at[k - 1, c],
            device_id={"mp": lax.rem(me + k, n)},
            device_id_type=MESH,
        )

    piece = span // 16

    @pl.loop(0, CHUNKS)
    def _(c):
        step(n - 1, c)
        for i in range(16):
            ks = pl.ds(pl.multiple_of(c * span + i * piece, piece), piece)
            share = jnp.sum(part[:, ks] * held[:, ks].astype(f32), axis=0, keepdims=True)
            gmine[c, i:i + 1, :] = share / gain[:, ks]
        gsend[c] = gmine[c].astype(jnp.bfloat16)

        @pl.loop(0, tiles_n)
        def _(i):
            ns = pl.ds(pl.multiple_of(i * tile_n, tile_n), tile_n)
            value = jnp.dot(held[:, cols(c)], w[cols(c), ns], preferred_element_type=f32)

            @pl.when(c == 0)
            def _():
                acc[:, ns] = value

            @pl.when(c > 0)
            def _():
                acc[:, ns] += value

            @pl.when(i == 0)
            def _():
                for k in range(1, n):
                    gain_copy(k, c).start()

    for h in range(heads):
        hs = slice(h * HEAD_DIM, (h + 1) * HEAD_DIM)
        x = acc[:, hs] + bias[:, hs]
        turned = x * cos[...] + pltpu.roll(x, HEAD_DIM // 2, 1) * sin[...]
        plain = lax.rem(me * heads + h, GROUP) == GROUP - 1
        qkv[:, hs] = jnp.where(plain, x, turned).astype(jnp.bfloat16)

    scale = scale_ref[:, :1]
    inner = jnp.zeros((rows, 1), f32)
    for c in range(CHUNKS):
        ks = slice(c * span, (c + 1) * span)
        ng[:, ks] = part[block(me), ks]
        for way, comes, slot in ((0, has_left, me + 1), (1, has_right, me)):
            @pl.when(comes)
            def _():
                transfer(way, run, slot, n - 1, c).wait_recv()
                ng[:, ks] += run[block(slot), ks].astype(f32)

        product = ng[:, ks] * tok[:, ks].astype(f32)
        inner = inner + jnp.sum(product * gain[:, ks], axis=1, keepdims=True)

    weight = scale * scale * scale * (inner / depth)
    for c in range(CHUNKS):
        ks = slice(c * span, (c + 1) * span)
        tg[:, ks] = scale * gain[:, ks] * ng[:, ks] - tok[:, ks].astype(f32) * weight

    for c in range(CHUNKS):
        total = gmine[c]
        for k in range(1, n):
            gain_copy(k, c).wait_recv()
            total = total + grecv[k - 1, c].astype(f32)
        for i in range(16):
            at = c * span + i * piece
            gg_ref[:, at:at + piece] = total[i:i + 1, :]

    @pl.loop(0, n)
    def _(j):
        @pl.loop(0, CHUNKS)
        def _(c):
            for way, goes in ((0, has_right), (1, has_left)):
                @pl.when(goes)
                def _():
                    transfer(way, held, 0, j, c).wait_send()

    for c in range(CHUNKS):
        for k in range(1, n):
            gain_copy(k, c).wait_send()


def finish(qkv, tg, gg, bg, qkv_h, tg_h, gg_h, bg_h, sem):
    moves = ((qkv, qkv_h), (tg, tg_h), (gg.at[0], gg_h), (bg.at[0], bg_h))
    copies = [pltpu.make_async_copy(src, dst, sem.at[i]) for i, (src, dst) in enumerate(moves)]
    for c in copies:
        c.start()
    for c in copies:
        c.wait()


def shards(n, tokens, norm_gain, qkv_weight, qkv_bias, qkv_grad):
    rows, depth = tokens.shape
    every, width = qkv_grad.shape
    cosine, sine = rope_tables(every, rows, SEQ_LEN // n)
    bf16, f32 = jnp.bfloat16, jnp.float32
    span = depth // CHUNKS
    dma = pltpu.SemaphoreType.DMA
    hbm = pl.BlockSpec(memory_space=pl.ANY)
    vmem = pl.BlockSpec(memory_space=pltpu.VMEM)
    results = pl.pallas_call(
        functools.partial(kernel, n),
        out_shape=(
            pltpu.VMEM((every, width), bf16),
            pltpu.VMEM((rows, depth), f32),
            pltpu.VMEM((1, depth), f32),
            pltpu.VMEM((1, width), f32),
        ),
        in_specs=[hbm] * 7,
        out_specs=[vmem] * 4,
        scratch_shapes=[
            pltpu.VMEM((rows, depth), bf16),
            pltpu.VMEM((1, depth), f32),
            pltpu.VMEM((depth, width), bf16),
            pltpu.VMEM((1, width), f32),
            pltpu.VMEM((every, width), bf16),
            pltpu.VMEM((every, HEAD_DIM), f32),
            pltpu.VMEM((every, HEAD_DIM), f32),
            pltpu.VMEM((every, width), bf16),
            pltpu.VMEM((every, depth), f32),
            pltpu.VMEM((every, depth), bf16),
            pltpu.VMEM((every + rows, depth), bf16),
            pltpu.VMEM((every, width), f32),
            pltpu.VMEM((rows, depth), f32),
            pltpu.VMEM((rows, HEAD_DIM), f32),
            pltpu.VMEM((CHUNKS, 16, span // 16), f32),
            pltpu.VMEM((CHUNKS, 16, span // 16), bf16),
            pltpu.VMEM((n - 1, CHUNKS, 16, span // 16), bf16),
            dma((6,)),
            dma((depth // TILE_K,)),
            dma((2, n, CHUNKS)),
            dma((2, n, CHUNKS)),
            dma((n - 1, CHUNKS)),
            dma((n - 1, CHUNKS)),
        ],
        compiler_params=pltpu.CompilerParams(
            collective_id=0, has_side_effects=True, vmem_limit_bytes=60000000
        ),
        cost_estimate=pl.CostEstimate(
            flops=4 * every * depth * width, bytes_accessed=2 * depth * width, transcendentals=0
        ),
    )(
        tokens, norm_gain, qkv_weight, qkv_bias, qkv_grad,
        jnp.asarray(cosine), jnp.asarray(sine),
    )
    return pl.pallas_call(
        finish,
        out_shape=(
            jax.ShapeDtypeStruct((every, width), bf16),
            jax.ShapeDtypeStruct((rows, depth), f32),
            jax.ShapeDtypeStruct((depth,), f32),
            jax.ShapeDtypeStruct((width,), f32),
        ),
        in_specs=[vmem] * 4,
        out_specs=[hbm] * 4,
        scratch_shapes=[dma((4,))],
        compiler_params=pltpu.CompilerParams(vmem_limit_bytes=1 << 20),
    )(*results)


def solution(mesh):
    in_specs = (P(("dp", "mp"), None), P(), P(None, "mp"), P("mp"), P("dp", "mp"))
    out_specs = (P("dp", "mp"), P(("dp", "mp"), None), P("dp"), P(("dp", "mp")))
    body = functools.partial(shards, mesh.shape["mp"])
    return jax.shard_map(body, mesh=mesh, in_specs=in_specs, out_specs=out_specs, check_vma=False)
```

profile of v0, /device:TPU:1, one launch (start us, length us, event | category | flops | bytes accessed | tf_op | source)
XLA Modules:
  0.0 373.6 jit_solution(5959841677799644388)
XLA Ops:
  0.6 371.7 %shard_map.102 = (bf16[512,640]{1,0:T(8,128)(2,1)S(1)}, f32[32,8192]{1,0:T(8,128)S(1)}, f32[1,8192]{1,0:T(1,128)S(1)}, f32[1,640]{1,0:T(1,128)S(1)}) custom-call(bf16[32,8192]{1,0:T(8,128)(2,1)} %tok_h.1, f32[8192]{0:T(1024)} %gain_h.1, bf16[8192,640]{1,0:T(8,128)(2,1)} %w_h.1, f32[640]{0:T(1024)} %bias_h.1, bf16[512,640]{1,0:T(8,128)(2,1)} %grad_h.1, ...), custom_call_target="tpu_custom_call" | custom-call | flops 10737418240 | bytes 10485760 | tf_op jit(solution)/shard_map/pallas_call | solution.py:293
  372.4 1.2 shard_map.103
where the time goes:
time: 378 us; the launch traced here: 374 us
  Pallas kernels  373 us (99%)
    pallas_call x1, Pallas kernels, shards(): pl.pallas_call(functools.partial(kernel, n), out_shape=(pltpu.VMEM((every...  372 us

commit v1 on v0

v1 whole, which is shorter than its diff:
```python
import functools

import jax
import jax.numpy as jnp
import numpy as np
from jax import lax
from jax.experimental import pallas as pl
from jax.experimental.pallas import tpu as pltpu
from jax.sharding import PartitionSpec as P

HEAD_DIM = 128
SEQ_LEN = 32768
GROUP = 10
MESH = pl.DeviceIdType.MESH
CHUNK = 512
WCHUNK = 256
TILE_N = 256


def rope_tables(rows, tok_dev, stride):
    half = HEAD_DIM // 2
    row = np.arange(rows)
    place = (row // tok_dev * stride + row % tok_dev).astype(np.float32)
    inverse = np.exp(
        -np.log(np.float32(1000000.0))
        * (np.float32(2.0) * np.arange(half).astype(np.float32) / np.float32(HEAD_DIM))
    ).astype(np.float32)
    angle = (place[:, None] * inverse[None, :]).astype(np.float32)
    cosine, sine = np.cos(angle).astype(np.float32), np.sin(angle).astype(np.float32)

    def by_column(t):
        t = t.reshape(rows // (2 * tok_dev), 2, tok_dev, HEAD_DIM)
        return np.ascontiguousarray(np.swapaxes(t, 0, 1)).reshape(2, rows // 2, HEAD_DIM)

    return by_column(np.concatenate([cosine, cosine], 1)), by_column(np.concatenate([-sine, sine], 1))


def kernel(
    nz, ndp,
    tok_h, gain_h, w_h, bias_h, grad_h, cos_h, sin_h,
    qkv, tg, gg_ref, bg_ref,
    tok, gain, w, bias, grad, cos, sin,
    low, lowx, nx, held, part, run, acc, cx, qt, qx, ng, fin, gtot, gx, grecv, gres, bacc,
    in_sem, w_sem, wx_s, wx_r, nx_s, nx_r, low_s, low_r, bias_s, bias_r,
    ag_s, ag_r, rs_s, rs_r, fin_s, fin_r, c_s, c_r, q_s, q_r,
    gx_s, gx_r, g1_s, g1_r, g2_s, g2_r,
):
    f32, bf16 = jnp.float32, jnp.bfloat16
    dp, mp = lax.axis_index("dp"), lax.axis_index("mp")
    n = 2 * nz
    z, yl, core = mp // 2, lax.rem(mp, 2), lax.rem(dp, 2)
    rows, depth = tok.shape
    half = depth // 2
    col = nz * rows
    width = grad.shape[1]
    heads = width // HEAD_DIM
    chunks = half // CHUNK
    wchunks = half // WCHUNK
    quarter = half // 4
    slab = depth // n

    def at(start, size, unit):
        return pl.ds(pl.multiple_of(start, unit), size)

    up = {"mp": lax.rem(z + 1, nz) * 2 + yl}
    down = {"mp": lax.rem(z + nz - 1, nz) * 2 + yl}
    pair = {"mp": mp + 1 - 2 * yl}
    far = {"dp": lax.rem(dp + ndp // 2, ndp), "mp": mp + 1 - 2 * yl}
    twin = {"dp": dp + 1 - 2 * core}
    along = (up, down)

    barrier = pltpu.get_barrier_semaphore()
    for there in (up, down, pair, far, twin):
        pl.semaphore_signal(barrier, inc=1, device_id=there, device_id_type=MESH)

    loads = []
    for i, (src, dst) in enumerate((
        (tok_h, tok), (gain_h, gain.at[0]), (grad_h, grad), (cos_h, cos), (sin_h, sin),
        (bias_h, bias.at[0, pl.ds(0, width)]),
    )):
        c = pltpu.make_async_copy(src, dst, in_sem.at[i])
        c.start()
        loads.append(c)

    def w_load(k):
        return pltpu.make_async_copy(
            w_h.at[at(core * half + k * CHUNK, CHUNK, CHUNK), :],
            w.at[at(k * CHUNK, CHUNK, CHUNK), pl.ds(0, width)],
            w_sem.at[k],
        )

    @pl.loop(0, chunks)
    def _(k):
        w_load(k).start()

    def remote(src, dst, send, recv, there):
        return pltpu.make_async_remote_copy(
            src_ref=src, dst_ref=dst, send_sem=send, recv_sem=recv, device_id=there, device_id_type=MESH
        )

    def w_send(i, there):
        return remote(
            w_h.at[at(core * half + i * WCHUNK, WCHUNK, WCHUNK), :],
            w.at[at(i * WCHUNK, WCHUNK, WCHUNK), pl.ds(width, width)],
            wx_s.at[i], wx_r.at[i], there,
        )

    mine = at(core * col, col, col)
    other = at((1 - core) * col, col, col)
    home = at(core * col + z * rows, rows, rows)

    def nx_send(q):
        ks = pl.ds(q * quarter, quarter)
        return remote(nx.at[:, ks], held.at[home, ks], nx_s.at[q], nx_r.at[q], twin)

    def ag(way, j, e):
        d = lax.rem(core + e // 4, 2)
        b = lax.rem(z + (nz - j if way == 0 else j), nz)
        ref = held.at[at(d * col + b * rows, rows, rows), at(lax.rem(e, 4) * quarter, quarter, quarter)]
        return remote(ref, ref, ag_s.at[way, j, e], ag_r.at[way, j, e], along[way])

    loads[0].wait()
    loads[1].wait()
    total = jnp.zeros((rows, 1), f32)
    for q in range(8):
        v = tok[:, q * quarter:(q + 1) * quarter].astype(f32)
        total = total + jnp.sum(v * v, axis=1, keepdims=True)
    scale = lax.rsqrt(total / depth + 1e-06)

    def normed(ks):
        return (tok[:, ks].astype(f32) * scale * gain[:, ks]).astype(bf16)

    for q in range(4):
        held[home, q * quarter:(q + 1) * quarter] = normed(at(core * half + q * quarter, quarter, quarter))
    pl.semaphore_wait(barrier, 5)
    for q in range(4):
        for way in range(2):
            ag(way, 0, q).start()
    remote(
        bias_h, bias.at[0, pl.ds(width, width)], bias_s.at[0], bias_r.at[0], pair
    ).start()
    for q in range(4):
        nx[:, q * quarter:(q + 1) * quarter] = normed(at((1 - core) * half + q * quarter, quarter, quarter))
        nx_send(q).start()

    @pl.loop(0, wchunks)
    def _(i):
        @pl.when((i == 0) | (lax.rem(i, 2) == 1))
        def _():
            w_send(i, far).start()

    for l in loads[2:]:
        l.wait()
    bacc[...] = jnp.zeros_like(bacc)

    @pl.loop(0, nz)
    def _(b):
        for side, y in ((0, yl), (1, 1 - yl)):
            here = at((2 * b + y) * rows, rows, rows)
            there = at(b * rows, rows, rows)
            cs, sn = cos[y, there, :], sin[y, there, :]
            for h in range(heads):
                hs = slice(h * HEAD_DIM, (h + 1) * HEAD_DIM)
                x = grad[here, hs].astype(f32)
                turned = x * cs - pltpu.roll(x, HEAD_DIM // 2, 1) * sn
                plain = lax.rem(mp * heads + h, GROUP) == GROUP - 1
                x = jnp.where(plain, x, turned)
                bacc[:, hs] += jnp.sum(x.reshape(rows // 8, 8, HEAD_DIM), axis=0)
                if side == 0:
                    low[at(core * col + b * rows, rows, rows), hs] = x.astype(bf16)
                else:
                    lowx[there, hs] = x.astype(bf16)

    own_cols, pair_cols = pl.ds(0, width), pl.ds(width, width)
    low_pair = remote(lowx, low.at[mine, pair_cols], low_s.at[0], low_r.at[0], pair)
    low_twin = remote(low.at[mine, own_cols], low.at[mine, own_cols], low_s.at[1], low_r.at[1], twin)
    low_fwd = remote(low.at[mine, pair_cols], low.at[mine, pair_cols], low_s.at[2], low_r.at[2], twin)
    low_pair.start()
    low_twin.start()
    for q in range(4):
        nx_send(q).wait_recv()
        for way in range(2):
            ag(way, 0, 4 + q).start()

    @pl.loop(0, wchunks)
    def _(i):
        @pl.when((i > 0) & (lax.rem(i, 2) == 0))
        def _():
            w_send(i, pair).start()

    bg_ref[...] = jnp.sum(bacc[...], axis=0, keepdims=True)

    def cols(k):
        return at(k * CHUNK, CHUNK, CHUNK)

    def backward(k):
        w_send(2 * k, pair).wait_recv()
        w_send(2 * k + 1, pair).wait_recv()
        part[:, cols(k)] = lax.dot_general(
            low[...], w[cols(k), :], (((1,), (1,)), ((), ())), preferred_element_type=f32
        )

    def hops(way, k):
        return jnp.where(lax.rem(k, 2) == way, 4, 3)

    def rs(way, j, k):
        return remote(
            run.at[way, j, :, cols(k)], run.at[way, j + 1, :, cols(k)],
            rs_s.at[way, j, k], rs_r.at[way, j, k], along[way],
        )

    def rs_step(way, j, k):
        left = hops(way, k) - j
        t = lax.rem(z + (left if way == 0 else nz - left), nz)
        if j > 0:
            rs(way, j - 1, k).wait_recv()
        for d in range(2):
            ds = pl.ds(d * rows, rows)
            v = part[at(d * col + t * rows, rows, rows), cols(k)]
            if j > 0:
                v = v + run[way, j, ds, cols(k)].astype(f32)
            run[way, j, ds, cols(k)] = v.astype(bf16)
        rs(way, j, k).start()

    def fin_send(k):
        return remote(
            fin.at[:, cols(k)], ng.at[:, at(core * half + k * CHUNK, CHUNK, CHUNK)], fin_s.at[k], fin_r.at[k], twin
        )

    def rs_final(k):
        for way in range(2):
            rs(way, hops(way, k) - 1, k).wait_recv()
        for d, to in ((core, None), (1 - core, fin)):
            ds = at(d * rows, rows, rows)
            v = part[at(d * col + z * rows, rows, rows), cols(k)]
            for way in range(2):
                v = v + run[way, hops(way, k), ds, cols(k)].astype(f32)
            if to is None:
                ng[:, at(core * half + k * CHUNK, CHUNK, CHUNK)] = v
            else:
                fin[:, cols(k)] = v
        fin_send(k).start()

    def gain_share(k):
        full = at(core * half + k * CHUNK, CHUNK, CHUNK)
        for ds, to, ks in ((mine, gtot, full), (other, gx, cols(k))):
            share = jnp.sum(part[ds, cols(k)] * held[ds, cols(k)].astype(f32), axis=0, keepdims=True)
            to[:, ks] = share / gain[:, full]

    gx_send = remote(gx, gtot.at[:, at(core * half, half, half)], gx_s.at[0], gx_r.at[0], twin)

    def slab_of(i):
        return at(i * slab, slab, slab)

    def g1(k):
        to = lax.rem(mp + k, n)
        return remote(gtot.at[:, slab_of(to)], grecv.at[k - 1], g1_s.at[k - 1], g1_r.at[k - 1], {"mp": to})

    def g2(k):
        to = lax.rem(mp + k, n)
        return remote(
            gres.at[:, slab_of(mp)], gres.at[:, slab_of(mp)], g2_s.at[k - 1], g2_r.at[k - 1], {"mp": to}
        )

    def tile(t):
        return at(t * TILE_N, TILE_N, TILE_N)

    def c_send(t):
        return remote(acc.at[other, tile(t)], cx.at[:, tile(t)], c_s.at[t], c_r.at[t], twin)

    def forward(t):
        acc[:, tile(t)] = jnp.dot(held[...], w[:, tile(t)], preferred_element_type=f32)
        c_send(t).start()

    def q_send(h):
        return remote(
            qt.at[:, at(width + h * HEAD_DIM, HEAD_DIM, HEAD_DIM)], qx.at[:, at(h * HEAD_DIM, HEAD_DIM, HEAD_DIM)],
            q_s.at[h], q_r.at[h], pair,
        )

    def joined(t):
        c_send(t).wait_recv()
        for i in range(TILE_N // HEAD_DIM):
            h = t * (TILE_N // HEAD_DIM) + i
            hs = at(h * HEAD_DIM, HEAD_DIM, HEAD_DIM)
            x = acc[mine, hs] + cx[:, hs] + bias[:, hs]
            turned = x * cos[yl] + pltpu.roll(x, HEAD_DIM // 2, 1) * sin[yl]
            whole = jnp.where(h < heads, mp * heads + h, (mp + 1 - 2 * yl) * heads + h - heads)
            qt[:, hs] = jnp.where(lax.rem(whole, GROUP) == GROUP - 1, x, turned).astype(bf16)

            @pl.when(h >= heads)
            def _():
                q_send(h - heads).start()

    @pl.loop(0, 24)
    def _(i):
        j, e = 1 + i // 8, lax.rem(i, 8)
        for way in range(2):
            ag(way, j - 1, e).wait_recv()

            @pl.when((j < 3) | (lax.rem(e, 2) == way))
            def _():
                ag(way, j, e).start()

        @pl.when(i == 5)
        def _():
            low_pair.wait_recv()
            low_fwd.start()

        @pl.when(i == 7)
        def _():
            for k in range(chunks):
                w_load(k).wait()
            low_twin.wait_recv()
            low_fwd.wait_recv()

        @pl.when((i == 8) | (i == 12) | (i == 17) | (i == 22))
        def _():
            backward((i - 8) // 4)

    for k in range(2):
        for way in range(2):
            rs_step(way, 0, k)
    for e in range(8):
        ag(e % 2, 3, e).wait_recv()
    bias_wait = remote(bias_h, bias.at[0, pl.ds(width, width)], bias_s.at[0], bias_r.at[0], pair)
    bias_wait.wait_recv()
    for k in range(2):
        gain_share(k)

    @pl.loop(0, chunks + 3)
    def _(s):
        k3, k2, k1, k0 = s - 2, s - 1, s, s + 2

        for way in range(2):
            @pl.when((k3 >= 0) & (k3 < chunks) & (lax.rem(k3 + 2, 2) == way))
            def _():
                rs_step(way, 3, k3)

        for k, j in ((k2, 2), (k1, 1)):
            @pl.when((k >= 0) & (k < chunks))
            def _():
                for way in range(2):
                    rs_step(way, j, k)

        @pl.when((k0 >= 4) & (k0 < chunks))
        def _():
            backward(k0)

        @pl.when(k0 < chunks)
        def _():
            for way in range(2):
                rs_step(way, 0, k0)
            gain_share(k0)

        @pl.when(k0 == chunks - 1)
        def _():
            gx_send.start()

        @pl.when(s >= 3)
        def _():
            rs_final(s - 3)

        @pl.when((s == 2) | (s == 3) | ((s >= 6) & (s <= 8)))
        def _():
            joined(jnp.where(s < 4, s - 2, s - 4))

        @pl.when((s == 1) | (s == 2) | ((s >= 5) & (s <= 7)))
        def _():
            forward(jnp.where(s < 4, s - 1, s - 3))

        @pl.when(s == 6)
        def _():
            gx_send.wait_recv()
            for k in range(1, n):
                g1(k).start()

        @pl.when(s == 8)
        def _():
            share = gtot[:, slab_of(mp)]
            for k in range(1, n):
                g1(k).wait_recv()
                share = share + grecv[k - 1]
            gres[:, slab_of(mp)] = share
            for k in range(1, n):
                g2(k).start()

    for h in range(heads):
        q_send(h).wait_recv()
    for b in range(nz):
        there = pl.ds(b * rows, rows)
        qkv[at((2 * b + yl) * rows, rows, rows), :] = qt[there, pl.ds(0, width)]
        qkv[at((2 * b + 1 - yl) * rows, rows, rows), :] = qx[there, :]
    for k in range(1, n):
        g2(k).wait_recv()
    gg_ref[...] = gres[...]

    for k in range(chunks):
        fin_send(k).wait_recv()
    inner = jnp.zeros((rows, 1), f32)
    for q in range(8):
        ks = slice(q * quarter, (q + 1) * quarter)
        inner = inner + jnp.sum(ng[:, ks] * tok[:, ks].astype(f32) * gain[:, ks], axis=1, keepdims=True)
    weight = scale * scale * scale * (inner / depth)
    for q in range(8):
        ks = slice(q * quarter, (q + 1) * quarter)
        tg[:, ks] = scale * gain[:, ks] * ng[:, ks] - tok[:, ks].astype(f32) * weight

    bias_wait.wait_send()
    low_pair.wait_send()
    low_twin.wait_send()
    low_fwd.wait_send()
    gx_send.wait_send()
    for q in range(4):
        nx_send(q).wait_send()

    @pl.loop(0, wchunks)
    def _(i):
        w_send(i, pair).wait_send()

    @pl.loop(0, 4)
    def _(j):
        @pl.loop(0, 8)
        def _(e):
            for way in range(2):
                @pl.when((j < 3) | (lax.rem(e, 2) == way))
                def _():
                    ag(way, j, e).wait_send()
                    rs(way, j, e).wait_send()

    for k in range(chunks):
        fin_send(k).wait_send()
    for t in range(2 * width // TILE_N):
        c_send(t).wait_send()
    for h in range(heads):
        q_send(h).wait_send()
    for k in range(1, n):
        g1(k).wait_send()
        g2(k).wait_send()


def finish(qkv, tg, gg, bg, qkv_h, tg_h, gg_h, bg_h, sem):
    moves = ((qkv, qkv_h), (tg, tg_h), (gg.at[0], gg_h), (bg.at[0], bg_h))
    copies = [pltpu.make_async_copy(src, dst, sem.at[i]) for i, (src, dst) in enumerate(moves)]
    for c in copies:
        c.start()
    for c in copies:
        c.wait()


def shards(n, ndp, tokens, norm_gain, qkv_weight, qkv_bias, qkv_grad):
    rows, depth = tokens.shape
    every, width = qkv_grad.shape
    cosine, sine = rope_tables(every, rows, SEQ_LEN // n)
    bf16, f32 = jnp.bfloat16, jnp.float32
    half, col, nz = depth // 2, every // 2, n // 2
    chunks, wchunks, heads = half // CHUNK, half // WCHUNK, width // HEAD_DIM
    tiles = 2 * width // TILE_N
    dma = pltpu.SemaphoreType.DMA
    vm = pltpu.VMEM
    hbm = pl.BlockSpec(memory_space=pl.ANY)
    vmem = pl.BlockSpec(memory_space=pltpu.VMEM)
    results = pl.pallas_call(
        functools.partial(kernel, nz, ndp),
        out_shape=(
            vm((every, width), bf16),
            vm((rows, depth), f32),
            vm((1, depth), f32),
            vm((1, width), f32),
        ),
        in_specs=[hbm] * 7,
        out_specs=[vmem] * 4,
        scratch_shapes=[
            vm((rows, depth), bf16),
            vm((1, depth), f32),
            vm((half, 2 * width), bf16),
            vm((1, 2 * width), f32),
            vm((every, width), bf16),
            vm((2, col, HEAD_DIM), f32),
            vm((2, col, HEAD_DIM), f32),
            vm((every, 2 * width), bf16),
            vm((col, width), bf16),
            vm((rows, half), bf16),
            vm((every, half), bf16),
            vm((every, half), f32),
            vm((2, 5, 2 * rows, half), bf16),
            vm((every, 2 * width), f32),
            vm((col, 2 * width), f32),
            vm((col, 2 * width), bf16),
            vm((col, width), bf16),
            vm((rows, depth), f32),
            vm((rows, half), f32),
            vm((1, depth), f32),
            vm((1, half), f32),
            vm((n - 1, 1, depth // n), f32),
            vm((1, depth), f32),
            vm((8, width), f32),
            dma((6,)), dma((chunks,)),
            dma((wchunks,)), dma((wchunks,)),
            dma((4,)), dma((4,)),
            dma((3,)), dma((3,)),
            dma((1,)), dma((1,)),
            dma((2, 4, 8)), dma((2, 4, 8)),
            dma((2, 4, chunks)), dma((2, 4, chunks)),
            dma((chunks,)), dma((chunks,)),
            dma((tiles,)), dma((tiles,)),
            dma((heads,)), dma((heads,)),
            dma((1,)), dma((1,)),
            dma((n - 1,)), dma((n - 1,)),
            dma((n - 1,)), dma((n - 1,)),
        ],
        compiler_params=pltpu.CompilerParams(
            collective_id=0, has_side_effects=True, vmem_limit_bytes=60000000
        ),
        cost_estimate=pl.CostEstimate(
            flops=4 * every * depth * width, bytes_accessed=2 * depth * width, transcendentals=0
        ),
    )(
        tokens, norm_gain, qkv_weight, qkv_bias, qkv_grad,
        jnp.asarray(cosine), jnp.asarray(sine),
    )
    return pl.pallas_call(
        finish,
        out_shape=(
            jax.ShapeDtypeStruct((every, width), bf16),
            jax.ShapeDtypeStruct((rows, depth), f32),
            jax.ShapeDtypeStruct((depth,), f32),
            jax.ShapeDtypeStruct((width,), f32),
        ),
        in_specs=[vmem] * 4,
        out_specs=[hbm] * 4,
        scratch_shapes=[dma((4,))],
        compiler_params=pltpu.CompilerParams(vmem_limit_bytes=1 << 20),
    )(*results)


def solution(mesh):
    in_specs = (P(("dp", "mp"), None), P(), P(None, "mp"), P("mp"), P("dp", "mp"))
    out_specs = (P("dp", "mp"), P(("dp", "mp"), None), P("dp"), P(("dp", "mp")))
    body = functools.partial(shards, mesh.shape["mp"], mesh.shape["dp"])
    return jax.shard_map(body, mesh=mesh, in_specs=in_specs, out_specs=out_specs, check_vma=False)
```

time: 378 us -> 107 us (0.28); the launches traced: 374 us -> 107 us
  Pallas kernels: 373 us -> 107 us
    pallas_call x1, Pallas kernels: 372 us -> 105 us  [shards(): pl.pallas_call(functools.partial(kernel, nz, ndp), out_shape=(vm((every,...]
where the time goes in v1:
time: 107 us
  Pallas kernels  107 us (100%)
    pallas_call x1, Pallas kernels, shards(): pl.pallas_call(functools.partial(kernel, nz, ndp), out_shape=(vm((every,...  105 us

profile of v1, /device:TPU:1, one launch (start us, length us, event | category | flops | bytes accessed | tf_op | source)
XLA Modules:
  0.0 107.2 jit_solution(6813268614398164172)
XLA Ops:
  0.6 105.3 %shard_map.102 = (bf16[512,640]{1,0:T(8,128)(2,1)S(1)}, f32[32,8192]{1,0:T(8,128)S(1)}, f32[1,8192]{1,0:T(1,128)S(1)}, f32[1,640]{1,0:T(1,128)S(1)}) custom-call(bf16[32,8192]{1,0:T(8,128)(2,1)} %tok_h.1, f32[8192]{0:T(1024)} %gain_h.1, bf16[8192,640]{1,0:T(8,128)(2,1)} %w_h.1, f32[640]{0:T(1024)} %bias_h.1, bf16[512,640]{1,0:T(8,128)(2,1)} %grad_h.1, ...), custom_call_target="tpu_custom_call" | custom-call | flops 10737418240 | bytes 10485760 | tf_op jit(solution)/shard_map/pallas_call | solution.py:463
  106.0 1.2 %shard_map.103 = (bf16[512,640]{1,0:T(8,128)(2,1)}, f32[32,8192]{1,0:T(8,128)}, f32[8192]{0:T(1024)}, f32[640]{0:T(1024)}) custom-call(bf16[512,640]{1,0:T(8,128)(2,1)S(1)} %get-tuple-element.8.qkv, f32[32,8192]{1,0:T(8,128)S(1)} %get-tuple-element.9.tg, f32[1,8192]{1,0:T(1,128)S(1)} %get-tuple-element.10.gg, f32[1,640]{1,0:T(1,128)S(1)} %get-tuple-element.11.bg), custom_call_target="tpu_custom_call" | custom-call | tf_op jit(solution)/shard_map/pallas_call | solution.py:522

commit v2 on v1

v2 whole, which is shorter than its diff:
```python
import functools

import jax
import jax.numpy as jnp
import numpy as np
from jax import lax
from jax.experimental import pallas as pl
from jax.experimental.pallas import tpu as pltpu
from jax.sharding import PartitionSpec as P

HEAD_DIM = 128
SEQ_LEN = 32768
GROUP = 10
MESH = pl.DeviceIdType.MESH
CHUNK = 512
WCHUNK = 256
TILE_N = 256


def rope_tables(rows, tok_dev, stride):
    half = HEAD_DIM // 2
    row = np.arange(rows)
    place = (row // tok_dev * stride + row % tok_dev).astype(np.float32)
    inverse = np.exp(
        -np.log(np.float32(1000000.0))
        * (np.float32(2.0) * np.arange(half).astype(np.float32) / np.float32(HEAD_DIM))
    ).astype(np.float32)
    angle = (place[:, None] * inverse[None, :]).astype(np.float32)
    cosine, sine = np.cos(angle).astype(np.float32), np.sin(angle).astype(np.float32)

    def by_column(t):
        t = t.reshape(rows // (2 * tok_dev), 2, tok_dev, HEAD_DIM)
        return np.ascontiguousarray(np.swapaxes(t, 0, 1)).reshape(2, rows // 2, HEAD_DIM)

    return np.stack([by_column(np.concatenate([cosine, cosine], 1)), by_column(np.concatenate([-sine, sine], 1))])


def kernel(
    nz, ndp,
    tok_h, gain_h, w_h, bias_h, grad_h, rope_h,
    qkv, tg, gg_ref, bg_ref,
    tok, gain, w, bias, grad, rope,
    low, lowx, nx, held, part, run, acc, cx, qt, qx, ng, fin, gtot, gx, grecv, gres, bacc,
    in_sem, send_sem, one_sem, low_r, wy_r, wx_r, ag_r, rs_r, c_r,
):
    f32, bf16 = jnp.float32, jnp.bfloat16
    dp, mp = lax.axis_index("dp"), lax.axis_index("mp")
    n = 2 * nz
    z, yl, core = mp // 2, lax.rem(mp, 2), lax.rem(dp, 2)
    nx_chips = ndp // 4
    row_of_x = dp // (2 * nx_chips) * (2 * nx_chips)
    x = lax.rem(dp // 2, nx_chips)
    odd = lax.rem(x, 2)
    rows, depth = tok.shape
    half = depth // 2
    col = nz * rows
    width = grad.shape[1]
    heads = width // HEAD_DIM
    chunks = half // CHUNK
    quarter = half // 4
    slab = depth // n

    def at(start, size, unit):
        return pl.ds(pl.multiple_of(start, unit), size)

    up = {"mp": lax.rem(z + 1, nz) * 2 + yl}
    down = {"mp": lax.rem(z + nz - 1, nz) * 2 + yl}
    pair = {"mp": mp + 1 - 2 * yl}
    far = {"dp": lax.rem(dp + ndp // 2, ndp), "mp": mp + 1 - 2 * yl}
    twin = {"dp": dp + 1 - 2 * core}
    east = {"dp": row_of_x + lax.rem(x + 1, nx_chips) * 2 + core}
    west = {"dp": row_of_x + lax.rem(x + nx_chips - 1, nx_chips) * 2 + core}
    along = (up, down)

    barrier = pltpu.get_barrier_semaphore()
    peers = (up, down, pair, far, twin, east, west)
    for there in peers:
        pl.semaphore_signal(barrier, inc=1, device_id=there, device_id_type=MESH)

    loads = []
    for i, (src, dst) in enumerate((
        (tok_h, tok), (gain_h, gain.at[0]), (grad_h, grad), (rope_h, rope),
        (bias_h, bias.at[0, pl.ds(0, width)]),
        (w_h.at[at(core * half, half, half), :], w.at[:, pl.ds(0, width)]),
    )):
        c = pltpu.make_async_copy(src, dst, in_sem.at[i])
        c.start()
        loads.append(c)

    def remote(src, dst, send, recv, there):
        return pltpu.make_async_remote_copy(
            src_ref=src, dst_ref=dst, send_sem=send_sem.at[send], recv_sem=recv,
            device_id=there, device_id_type=MESH,
        )

    own_cols, pair_cols = pl.ds(0, width), pl.ds(width, width)

    def w_send(a, there):
        i = 2 * a + odd
        return remote(
            w_h.at[at(core * half + i * WCHUNK, WCHUNK, WCHUNK), :],
            w.at[at(i * WCHUNK, WCHUNK, WCHUNK), pair_cols], 0, wy_r.at[a], there,
        )

    def w_pass(a):
        ref = w.at[at((2 * a + odd) * WCHUNK, WCHUNK, WCHUNK), pair_cols]
        return remote(ref, ref, 1, wx_r.at[a], east if a % 2 == 0 else west)

    def w_come(k):
        ref = w.at[at((2 * k + 1 - odd) * WCHUNK, WCHUNK, WCHUNK), pair_cols]
        return remote(ref, ref, 1, wx_r.at[k], east)

    mine = at(core * col, col, col)
    other = at((1 - core) * col, col, col)
    home = at(core * col + z * rows, rows, rows)
    nx_send = remote(nx, held.at[home, :], 2, one_sem.at[0], twin)

    def ag(way, j, e):
        d = lax.rem(core + e // 4, 2)
        b = lax.rem(z + (nz - j if way == 0 else j), nz)
        ref = held.at[at(d * col + b * rows, rows, rows), at(lax.rem(e, 4) * quarter, quarter, quarter)]
        place = j * 8 + jnp.where(j < 3, e, e // 2)
        return remote(ref, ref, 3, ag_r.at[way, place], along[way])

    loads[0].wait()
    loads[1].wait()
    total = jnp.zeros((rows, 1), f32)
    for q in range(8):
        v = tok[:, q * quarter:(q + 1) * quarter].astype(f32)
        total = total + jnp.sum(v * v, axis=1, keepdims=True)
    scale = lax.rsqrt(total / depth + 1e-06)

    def normed(ks):
        return (tok[:, ks].astype(f32) * scale * gain[:, ks]).astype(bf16)

    for q in range(4):
        held[home, q * quarter:(q + 1) * quarter] = normed(at(core * half + q * quarter, quarter, quarter))
    for q in range(4):
        nx[:, q * quarter:(q + 1) * quarter] = normed(at((1 - core) * half + q * quarter, quarter, quarter))
    pl.semaphore_wait(barrier, len(peers))
    for q in range(4):
        for way in range(2):
            ag(way, 0, q).start()
    nx_send.start()
    bias_send = remote(bias_h, bias.at[0, pair_cols], 4, one_sem.at[1], pair)
    bias_send.start()
    for a in (0, 1, 3, 5, 7):
        w_send(a, far).start()

    loads[2].wait()
    loads[3].wait()
    bacc[...] = jnp.zeros_like(bacc)

    @pl.loop(0, nz)
    def _(b):
        for side, y in ((0, yl), (1, 1 - yl)):
            here = at((2 * b + y) * rows, rows, rows)
            there = at(b * rows, rows, rows)
            cs, sn = rope[0, y, there, :], rope[1, y, there, :]
            for h in range(heads):
                hs = slice(h * HEAD_DIM, (h + 1) * HEAD_DIM)
                v = grad[here, hs].astype(f32)
                turned = v * cs - pltpu.roll(v, HEAD_DIM // 2, 1) * sn
                plain = lax.rem(mp * heads + h, GROUP) == GROUP - 1
                v = jnp.where(plain, v, turned)
                bacc[:, hs] += jnp.sum(v.reshape(rows // 8, 8, HEAD_DIM), axis=0)
                if side == 0:
                    low[at(core * col + b * rows, rows, rows), hs] = v.astype(bf16)
                else:
                    lowx[there, hs] = v.astype(bf16)

    low_pair = remote(lowx, low.at[mine, pair_cols], 5, low_r.at[0], pair)
    low_twin = remote(low.at[mine, own_cols], low.at[mine, own_cols], 5, low_r.at[1], twin)
    low_fwd = remote(low.at[mine, pair_cols], low.at[mine, pair_cols], 5, low_r.at[2], twin)
    low_pair.start()
    low_twin.start()
    for a in (2, 4, 6):
        w_send(a, pair).start()
    nx_send.wait_recv()
    for q in range(4):
        for way in range(2):
            ag(way, 0, 4 + q).start()
    bg_ref[...] = jnp.sum(bacc[...], axis=0, keepdims=True)

    def cols(k):
        return at(k * CHUNK, CHUNK, CHUNK)

    def backward(k):
        w_come(k).wait_recv()
        part[:, cols(k)] = lax.dot_general(
            low[...], w[cols(k), :], (((1,), (1,)), ((), ())), preferred_element_type=f32
        )

    def rs(way, j, k):
        place = j * 8 + jnp.where(j < 3, k, k // 2)
        return remote(
            run.at[way, j, :, cols(k)], run.at[way, j + 1, :, cols(k)], 6, rs_r.at[way, place], along[way]
        )

    def hops(way, k):
        return jnp.where(lax.rem(k, 2) == way, 4, 3)

    def rs_step(way, j, k, first):
        left = hops(way, k) - j
        t = lax.rem(z + (left if way == 0 else nz - left), nz)
        if not first:
            rs(way, j - 1, k).wait_recv()
        for d in range(2):
            ds = pl.ds(d * rows, rows)
            v = part[at(d * col + t * rows, rows, rows), cols(k)]
            if not first:
                v = v + run[way, j, ds, cols(k)].astype(f32)
            run[way, j, ds, cols(k)] = v.astype(bf16)
        rs(way, j, k).start()

    def fin_send(k):
        return remote(
            fin.at[:, cols(k)], ng.at[:, at(core * half + k * CHUNK, CHUNK, CHUNK)], 7, one_sem.at[2], twin
        )

    def rs_final(k):
        for way in range(2):
            rs(way, hops(way, k) - 1, k).wait_recv()
        for d, to in ((core, None), (1 - core, fin)):
            ds = at(d * rows, rows, rows)
            v = part[at(d * col + z * rows, rows, rows), cols(k)]
            for way in range(2):
                v = v + run[way, hops(way, k), ds, cols(k)].astype(f32)
            if to is None:
                ng[:, at(core * half + k * CHUNK, CHUNK, CHUNK)] = v
            else:
                fin[:, cols(k)] = v
        fin_send(k).start()

    def gain_share(k):
        full = at(core * half + k * CHUNK, CHUNK, CHUNK)
        for ds, to, ks in ((mine, gtot, full), (other, gx, cols(k))):
            share = jnp.sum(part[ds, cols(k)] * held[ds, cols(k)].astype(f32), axis=0, keepdims=True)
            to[:, ks] = share / gain[:, full]

    gx_send = remote(gx, gtot.at[:, at(core * half, half, half)], 8, one_sem.at[3], twin)

    def slab_of(i):
        return at(i * slab, slab, slab)

    def g1(k):
        to = lax.rem(mp + k, n)
        return remote(gtot.at[:, slab_of(to)], grecv.at[k - 1], 9, one_sem.at[4], {"mp": to})

    def g2(k):
        to = lax.rem(mp + k, n)
        return remote(gres.at[:, slab_of(mp)], gres.at[:, slab_of(mp)], 10, one_sem.at[5], {"mp": to})

    g1_all = remote(grecv, grecv, 9, one_sem.at[4], up)
    g2_all = remote(gres.at[:, pl.ds(0, (n - 1) * slab)], gres.at[:, pl.ds(0, (n - 1) * slab)], 10, one_sem.at[5], up)

    def tile(t):
        return at(t * TILE_N, TILE_N, TILE_N)

    def c_send(t):
        return remote(acc.at[other, tile(t)], cx.at[:, tile(t)], 11, c_r.at[t], twin)

    def forward(t):
        acc[:, tile(t)] = jnp.dot(held[...], w[:, tile(t)], preferred_element_type=f32)
        c_send(t).start()

    def q_send(h):
        return remote(
            qt.at[:, at(width + h * HEAD_DIM, HEAD_DIM, HEAD_DIM)], qx.at[:, at(h * HEAD_DIM, HEAD_DIM, HEAD_DIM)],
            12, one_sem.at[6], pair,
        )

    q_all = remote(qx, qx, 12, one_sem.at[6], pair)

    def joined(t):
        c_send(t).wait_recv()
        for i in range(TILE_N // HEAD_DIM):
            h = t * (TILE_N // HEAD_DIM) + i
            hs = at(h * HEAD_DIM, HEAD_DIM, HEAD_DIM)
            v = acc[mine, hs] + cx[:, hs] + bias[:, hs]
            turned = v * rope[0, yl] + pltpu.roll(v, HEAD_DIM // 2, 1) * rope[1, yl]
            whole = jnp.where(h < heads, mp * heads + h, (mp + 1 - 2 * yl) * heads + h - heads)
            qt[:, hs] = jnp.where(lax.rem(whole, GROUP) == GROUP - 1, v, turned).astype(bf16)

            @pl.when(h >= heads)
            def _():
                q_send(h - heads).start()

    passes = (3, 8, 10, 13, 15, 18, 20, 23)
    early = (11, 16, 18, 21, 23)

    @pl.loop(0, 24)
    def _(i):
        j, e = 1 + i // 8, lax.rem(i, 8)
        for way in range(2):
            ag(way, j - 1, e).wait_recv()

            @pl.when((j < 3) | (lax.rem(e, 2) == way))
            def _():
                ag(way, j, e).start()

        for a, step in enumerate(passes):
            @pl.when(i == step)
            def _():
                w_send(a, pair).wait_recv()
                w_pass(a).start()

        @pl.when(i == 6)
        def _():
            low_pair.wait_recv()
            low_fwd.start()

        @pl.when(i == 9)
        def _():
            loads[5].wait()
            low_twin.wait_recv()
            low_fwd.wait_recv()

        k, due = 0, i == early[0]
        for m in range(1, len(early)):
            k, due = jnp.where(i >= early[m], m, k), due | (i == early[m])

        @pl.when(due)
        def _():
            backward(k)

    @pl.loop(0, chunks)
    def _(k):
        @pl.when(k >= len(early))
        def _():
            backward(k)

        for way in range(2):
            rs_step(way, 0, k, True)

    for e in range(8):
        ag(e % 2, 3, e).wait_recv()
    loads[4].wait()
    bias_send.wait_recv()

    @pl.loop(0, chunks)
    def _(k):
        gain_share(k)

    gx_send.start()

    @pl.loop(0, 20)
    def _(m):
        j, q = 1 + m // 8, lax.rem(m, 8)
        for way in range(2):
            rs_step(way, j, jnp.where(j < 3, q, 2 * q + way), False)

        @pl.when((m >= 2) & (m < 7))
        def _():
            joined(lax.rem(m, 5))

        @pl.when(m < 5)
        def _():
            forward(lax.rem(m + 2, 5))

        @pl.when(m == 1)
        def _():
            gx_send.wait_recv()
            for k in range(1, n):
                g1(k).start()

        @pl.when(m == 9)
        def _():
            g1_all.wait_recv()
            share = gtot[:, slab_of(mp)]
            for k in range(1, n):
                share = share + grecv[k - 1]
            gres[:, slab_of(mp)] = share
            for k in range(1, n):
                g2(k).start()

        @pl.when(m == 16)
        def _():
            q_all.wait_recv()
            for b in range(nz):
                there = pl.ds(b * rows, rows)
                qkv[at((2 * b + yl) * rows, rows, rows), :] = qt[there, own_cols]
                qkv[at((2 * b + 1 - yl) * rows, rows, rows), :] = qx[there, :]

    @pl.loop(0, chunks)
    def _(k):
        rs_final(k)

    g2_all.wait_recv()
    gg_ref[...] = gres[...]
    remote(fin, fin, 7, one_sem.at[2], twin).wait_recv()
    inner = jnp.zeros((rows, 1), f32)
    for q in range(8):
        ks = slice(q * quarter, (q + 1) * quarter)
        inner = inner + jnp.sum(ng[:, ks] * tok[:, ks].astype(f32) * gain[:, ks], axis=1, keepdims=True)
    weight = scale * scale * scale * (inner / depth)
    for q in range(8):
        ks = slice(q * quarter, (q + 1) * quarter)
        tg[:, ks] = scale * gain[:, ks] * ng[:, ks] - tok[:, ks].astype(f32) * weight

    def sent(ref, send):
        remote(ref, ref, send, one_sem.at[0], twin).wait_send()

    sent(w_h.at[pl.ds(0, half // 2), :], 0)
    sent(w_h.at[pl.ds(0, half // 2), :], 1)
    sent(nx, 2)
    moved = held.at[pl.ds(0, 7 * 2 * rows), :]
    sent(moved, 3)
    bias_send.wait_send()
    sent(w_h.at[pl.ds(0, 3 * col), :], 5)
    sent(moved, 6)
    sent(fin, 7)
    sent(gx, 8)
    sent(grecv, 9)
    sent(grecv, 10)
    sent(cx, 11)
    sent(qx, 12)


def finish(qkv, tg, gg, bg, qkv_h, tg_h, gg_h, bg_h, sem):
    moves = ((qkv, qkv_h), (tg, tg_h), (gg.at[0], gg_h), (bg.at[0], bg_h))
    copies = [pltpu.make_async_copy(src, dst, sem.at[i]) for i, (src, dst) in enumerate(moves)]
    for c in copies:
        c.start()
    for c in copies:
        c.wait()


def shards(n, ndp, tokens, norm_gain, qkv_weight, qkv_bias, qkv_grad):
    rows, depth = tokens.shape
    every, width = qkv_grad.shape
    rope = rope_tables(every, rows, SEQ_LEN // n)
    bf16, f32 = jnp.bfloat16, jnp.float32
    half, col, nz = depth // 2, every // 2, n // 2
    chunks = half // CHUNK
    tiles = 2 * width // TILE_N
    dma = pltpu.SemaphoreType.DMA
    vm = pltpu.VMEM
    hbm = pl.BlockSpec(memory_space=pl.ANY)
    vmem = pl.BlockSpec(memory_space=pltpu.VMEM)
    results = pl.pallas_call(
        functools.partial(kernel, nz, ndp),
        out_shape=(
            vm((every, width), bf16),
            vm((rows, depth), f32),
            vm((1, depth), f32),
            vm((1, width), f32),
        ),
        in_specs=[hbm] * 6,
        out_specs=[vmem] * 4,
        scratch_shapes=[
            vm((rows, depth), bf16),
            vm((1, depth), f32),
            vm((half, 2 * width), bf16),
            vm((1, 2 * width), f32),
            vm((every, width), bf16),
            vm((2, 2, col, HEAD_DIM), f32),
            vm((every, 2 * width), bf16),
            vm((col, width), bf16),
            vm((rows, half), bf16),
            vm((every, half), bf16),
            vm((every, half), f32),
            vm((2, 5, 2 * rows, half), bf16),
            vm((every, 2 * width), f32),
            vm((col, 2 * width), f32),
            vm((col, 2 * width), bf16),
            vm((col, width), bf16),
            vm((rows, depth), f32),
            vm((rows, half), f32),
            vm((1, depth), f32),
            vm((1, half), f32),
            vm((n - 1, 1, depth // n), f32),
            vm((1, depth), f32),
            vm((8, width), f32),
            dma((6,)),
            dma((13,)),
            dma((7,)),
            dma((3,)),
            dma((chunks,)),
            dma((chunks,)),
            dma((2, 28)),
            dma((2, 28)),
            dma((tiles,)),
        ],
        compiler_params=pltpu.CompilerParams(
            collective_id=0, has_side_effects=True, vmem_limit_bytes=60000000
        ),
        cost_estimate=pl.CostEstimate(
            flops=4 * every * depth * width, bytes_accessed=2 * depth * width, transcendentals=0
        ),
    )(
        tokens, norm_gain, qkv_weight, qkv_bias, qkv_grad,
        jnp.asarray(rope),
    )
    return pl.pallas_call(
        finish,
        out_shape=(
            jax.ShapeDtypeStruct((every, width), bf16),
            jax.ShapeDtypeStruct((rows, depth), f32),
            jax.ShapeDtypeStruct((depth,), f32),
            jax.ShapeDtypeStruct((width,), f32),
        ),
        in_specs=[vmem] * 4,
        out_specs=[hbm] * 4,
        scratch_shapes=[dma((4,))],
        compiler_params=pltpu.CompilerParams(vmem_limit_bytes=1 << 20),
    )(*results)


def solution(mesh):
    in_specs = (P(("dp", "mp"), None), P(), P(None, "mp"), P("mp"), P("dp", "mp"))
    out_specs = (P("dp", "mp"), P(("dp", "mp"), None), P("dp"), P(("dp", "mp")))
    body = functools.partial(shards, mesh.shape["mp"], mesh.shape["dp"])
    return jax.shard_map(body, mesh=mesh, in_specs=in_specs, out_specs=out_specs, check_vma=False)
```

time: 107 us -> 95.7 us (0.89)
  Pallas kernels: 107 us -> 95 us
    pallas_call x1, Pallas kernels: 105 us -> 93.7 us  [shards(): pl.pallas_call(functools.partial(kernel, nz, ndp), out_shape=(vm((every,...]
where the time goes in v2:
time: 95.7 us; the launch traced here: 95.6 us
  Pallas kernels  95 us (99%)
    pallas_call x1, Pallas kernels, shards(): pl.pallas_call(functools.partial(kernel, nz, ndp), out_shape=(vm((every,...  93.7 us

profile of v2, /device:TPU:1, one launch (start us, length us, event | category | flops | bytes accessed | tf_op | source)
XLA Modules:
  0.0 95.6 jit_solution(3300314445911263915)
XLA Ops:
  0.6 93.7 %shard_map.93 = (bf16[512,640]{1,0:T(8,128)(2,1)S(1)}, f32[32,8192]{1,0:T(8,128)S(1)}, f32[1,8192]{1,0:T(1,128)S(1)}, f32[1,640]{1,0:T(1,128)S(1)}) custom-call(bf16[32,8192]{1,0:T(8,128)(2,1)} %tok_h.1, f32[8192]{0:T(1024)} %gain_h.1, bf16[8192,640]{1,0:T(8,128)(2,1)} %w_h.1, f32[640]{0:T(1024)} %bias_h.1, bf16[512,640]{1,0:T(8,128)(2,1)} %grad_h.1, ...), custom_call_target="tpu_custom_call" | custom-call | flops 10737418240 | bytes 10485760 | tf_op jit(solution)/shard_map/pallas_call | solution.py:441
  94.4 1.2 %shard_map.94 = (bf16[512,640]{1,0:T(8,128)(2,1)}, f32[32,8192]{1,0:T(8,128)}, f32[8192]{0:T(1024)}, f32[640]{0:T(1024)}) custom-call(bf16[512,640]{1,0:T(8,128)(2,1)S(1)} %get-tuple-element.8.qkv, f32[32,8192]{1,0:T(8,128)S(1)} %get-tuple-element.9.tg, f32[1,8192]{1,0:T(1,128)S(1)} %get-tuple-element.10.gg, f32[1,640]{1,0:T(1,128)S(1)} %get-tuple-element.11.bg), custom_call_target="tpu_custom_call" | custom-call | tf_op jit(solution)/shard_map/pallas_call | solution.py:495

commit v3 on v2

--- a/solution.py
+++ b/solution.py
@@ -40,12 +40,11 @@
     tok_h, gain_h, w_h, bias_h, grad_h, rope_h,
     qkv, tg, gg_ref, bg_ref,
     tok, gain, w, bias, grad, rope,
-    low, lowx, nx, held, part, run, acc, cx, qt, qx, ng, fin, gtot, gx, grecv, gres, bacc,
-    in_sem, send_sem, one_sem, low_r, wy_r, wx_r, ag_r, rs_r, c_r,
+    low, lowx, nx, held, part, run, rfin, acc, cx, qt, qx, ng, gtot, gx, gy, grecv, gres, bacc,
+    in_sem, send_sem, one_sem, low_r, wy_r, wx_r, ag_r, rs_r, end_r, c_r,
 ):
     f32, bf16 = jnp.float32, jnp.bfloat16
     dp, mp = lax.axis_index("dp"), lax.axis_index("mp")
-    n = 2 * nz
     z, yl, core = mp // 2, lax.rem(mp, 2), lax.rem(dp, 2)
     nx_chips = ndp // 4
     row_of_x = dp // (2 * nx_chips) * (2 * nx_chips)
@@ -58,7 +57,7 @@
     heads = width // HEAD_DIM
     chunks = half // CHUNK
     quarter = half // 4
-    slab = depth // n
+    slab = half // nz
 
     def at(start, size, unit):
         return pl.ds(pl.multiple_of(start, unit), size)
@@ -119,7 +118,8 @@
         d = lax.rem(core + e // 4, 2)
         b = lax.rem(z + (nz - j if way == 0 else j), nz)
         ref = held.at[at(d * col + b * rows, rows, rows), at(lax.rem(e, 4) * quarter, quarter, quarter)]
-        place = j * 8 + jnp.where(j < 3, e, e // 2)
+        on = jnp.where(lax.rem(e, 2) == way, 16 + e // 2, 20)
+        place = jnp.where(j < 2, j * 8 + e, jnp.where(j == 2, on, 20))
         return remote(ref, ref, 3, ag_r.at[way, place], along[way])
 
     loads[0].wait()
@@ -192,9 +192,16 @@
         )
 
     def rs(way, j, k):
-        place = j * 8 + jnp.where(j < 3, k, k // 2)
+        place = j * 8 + jnp.where(j < 2, k, k // 2)
         return remote(
             run.at[way, j, :, cols(k)], run.at[way, j + 1, :, cols(k)], 6, rs_r.at[way, place], along[way]
+        )
+
+    def rs_end(way, j, k, d):
+        return remote(
+            run.at[way, j, pl.ds(d * rows, rows), cols(k)],
+            rfin.at[way, :, at(core * half + k * CHUNK, CHUNK, CHUNK)],
+            6, end_r.at[way, core, j - 2], dict(along[way], dp=dp - core + d),
         )
 
     def hops(way, k):
@@ -211,26 +218,29 @@
             if not first:
                 v = v + run[way, j, ds, cols(k)].astype(f32)
             run[way, j, ds, cols(k)] = v.astype(bf16)
-        rs(way, j, k).start()
-
-    def fin_send(k):
-        return remote(
-            fin.at[:, cols(k)], ng.at[:, at(core * half + k * CHUNK, CHUNK, CHUNK)], 7, one_sem.at[2], twin
-        )
-
-    def rs_final(k):
+        if first:
+            rs(way, j, k).start()
+            return
+
+        @pl.when(left > 1)
+        def _():
+            rs(way, j, k).start()
+
+        @pl.when(left == 1)
+        def _():
+            for d in range(2):
+                rs_end(way, j, k, d).start()
+
+    own_half = at(core * half, half, half)
+    swap = remote(
+        part.at[at((1 - core) * col + z * rows, rows, rows), :], ng.at[:, own_half], 7, one_sem.at[2], twin
+    )
+
+    def ended(group):
         for way in range(2):
-            rs(way, hops(way, k) - 1, k).wait_recv()
-        for d, to in ((core, None), (1 - core, fin)):
-            ds = at(d * rows, rows, rows)
-            v = part[at(d * col + z * rows, rows, rows), cols(k)]
-            for way in range(2):
-                v = v + run[way, hops(way, k), ds, cols(k)].astype(f32)
-            if to is None:
-                ng[:, at(core * half + k * CHUNK, CHUNK, CHUNK)] = v
-            else:
-                fin[:, cols(k)] = v
-        fin_send(k).start()
+            for side in range(2):
+                ref = rfin.at[way, :, pl.ds(0, half // 2)]
+                remote(ref, ref, 6, end_r.at[way, side, group], up).wait_recv()
 
     def gain_share(k):
         full = at(core * half + k * CHUNK, CHUNK, CHUNK)
@@ -238,21 +248,25 @@
             share = jnp.sum(part[ds, cols(k)] * held[ds, cols(k)].astype(f32), axis=0, keepdims=True)
             to[:, ks] = share / gain[:, full]
 
-    gx_send = remote(gx, gtot.at[:, at(core * half, half, half)], 8, one_sem.at[3], twin)
+    gx_send = remote(gx, gtot.at[:, own_half], 8, one_sem.at[3], twin)
+    gy_send = remote(gtot.at[:, at((1 - yl) * half, half, half)], gy, 13, one_sem.at[7], pair)
+    column_half = at(yl * half, half, half)
+    g3_send = remote(gres.at[:, column_half], gres.at[:, column_half], 14, one_sem.at[8], pair)
 
     def slab_of(i):
-        return at(i * slab, slab, slab)
+        return at(yl * half + i * slab, slab, slab)
 
     def g1(k):
-        to = lax.rem(mp + k, n)
-        return remote(gtot.at[:, slab_of(to)], grecv.at[k - 1], 9, one_sem.at[4], {"mp": to})
+        to = lax.rem(z + k, nz)
+        return remote(gtot.at[:, slab_of(to)], grecv.at[k - 1], 9, one_sem.at[4], {"mp": 2 * to + yl})
 
     def g2(k):
-        to = lax.rem(mp + k, n)
-        return remote(gres.at[:, slab_of(mp)], gres.at[:, slab_of(mp)], 10, one_sem.at[5], {"mp": to})
+        to = lax.rem(z + k, nz)
+        return remote(gres.at[:, slab_of(z)], gres.at[:, slab_of(z)], 10, one_sem.at[5], {"mp": 2 * to + yl})
 
     g1_all = remote(grecv, grecv, 9, one_sem.at[4], up)
-    g2_all = remote(gres.at[:, pl.ds(0, (n - 1) * slab)], gres.at[:, pl.ds(0, (n - 1) * slab)], 10, one_sem.at[5], up)
+    g2_ref = gres.at[:, pl.ds(0, (nz - 1) * slab)]
+    g2_all = remote(g2_ref, g2_ref, 10, one_sem.at[5], up)
 
     def tile(t):
         return at(t * TILE_N, TILE_N, TILE_N)
@@ -293,10 +307,9 @@
     def _(i):
         j, e = 1 + i // 8, lax.rem(i, 8)
         for way in range(2):
-            ag(way, j - 1, e).wait_recv()
-
             @pl.when((j < 3) | (lax.rem(e, 2) == way))
             def _():
+                ag(way, j - 1, e).wait_recv()
                 ag(way, j, e).start()
 
         for a, step in enumerate(passes):
@@ -333,8 +346,13 @@
         for way in range(2):
             rs_step(way, 0, k, True)
 
-    for e in range(8):
-        ag(e % 2, 3, e).wait_recv()
+    swap.start()
+    for q in range(4):
+        ks = pl.ds(q * quarter, quarter)
+        ng[:, at(core * half + q * quarter, quarter, quarter)] = part[home, ks]
+    for way in range(2):
+        ref = held.at[pl.ds(0, 2 * rows), :]
+        remote(ref, ref, 3, ag_r.at[way, 20], up).wait_recv()
     loads[4].wait()
     bias_send.wait_recv()
 
@@ -361,17 +379,23 @@
         @pl.when(m == 1)
         def _():
             gx_send.wait_recv()
-            for k in range(1, n):
+            gy_send.start()
+
+        @pl.when(m == 4)
+        def _():
+            gy_send.wait_recv()
+            gtot[:, column_half] += gy[...]
+            for k in range(1, nz):
                 g1(k).start()
 
-        @pl.when(m == 9)
+        @pl.when(m == 13)
         def _():
             g1_all.wait_recv()
-            share = gtot[:, slab_of(mp)]
-            for k in range(1, n):
+            share = gtot[:, slab_of(z)]
+            for k in range(1, nz):
                 share = share + grecv[k - 1]
-            gres[:, slab_of(mp)] = share
-            for k in range(1, n):
+            gres[:, slab_of(z)] = share
+            for k in range(1, nz):
                 g2(k).start()
 
         @pl.when(m == 16)
@@ -382,21 +406,27 @@
                 qkv[at((2 * b + yl) * rows, rows, rows), :] = qt[there, own_cols]
                 qkv[at((2 * b + 1 - yl) * rows, rows, rows), :] = qx[there, :]
 
-    @pl.loop(0, chunks)
-    def _(k):
-        rs_final(k)
-
     g2_all.wait_recv()
-    gg_ref[...] = gres[...]
-    remote(fin, fin, 7, one_sem.at[2], twin).wait_recv()
+    g3_send.start()
+    swap.wait_recv()
+    ended(0)
+    for q in range(2 * chunks):
+        ks = slice(q * CHUNK, (q + 1) * CHUNK)
+        ng[:, ks] += rfin[1 - q % 2, :, ks].astype(f32)
+    ended(1)
     inner = jnp.zeros((rows, 1), f32)
-    for q in range(8):
-        ks = slice(q * quarter, (q + 1) * quarter)
-        inner = inner + jnp.sum(ng[:, ks] * tok[:, ks].astype(f32) * gain[:, ks], axis=1, keepdims=True)
+    for q in range(2 * chunks):
+        ks = slice(q * CHUNK, (q + 1) * CHUNK)
+        v = ng[:, ks] + rfin[q % 2, :, ks].astype(f32)
+        ng[:, ks] = v
+        inner = inner + jnp.sum(v * tok[:, ks].astype(f32) * gain[:, ks], axis=1, keepdims=True)
     weight = scale * scale * scale * (inner / depth)
     for q in range(8):
         ks = slice(q * quarter, (q + 1) * quarter)
         tg[:, ks] = scale * gain[:, ks] * ng[:, ks] - tok[:, ks].astype(f32) * weight
+
+    g3_send.wait_recv()
+    gg_ref[...] = gres[...]
 
     def sent(ref, send):
         remote(ref, ref, send, one_sem.at[0], twin).wait_send()
@@ -409,12 +439,14 @@
     bias_send.wait_send()
     sent(w_h.at[pl.ds(0, 3 * col), :], 5)
     sent(moved, 6)
-    sent(fin, 7)
+    swap.wait_send()
     sent(gx, 8)
     sent(grecv, 9)
     sent(grecv, 10)
     sent(cx, 11)
     sent(qx, 12)
+    gy_send.wait_send()
+    g3_send.wait_send()
 
 
 def finish(qkv, tg, gg, bg, qkv_h, tg_h, gg_h, bg_h, sem):
@@ -460,26 +492,28 @@
             vm((rows, half), bf16),
             vm((every, half), bf16),
             vm((every, half), f32),
-            vm((2, 5, 2 * rows, half), bf16),
+            vm((2, 4, 2 * rows, half), bf16),
+            vm((2, rows, depth), bf16),
             vm((every, 2 * width), f32),
             vm((col, 2 * width), f32),
             vm((col, 2 * width), bf16),
             vm((col, width), bf16),
             vm((rows, depth), f32),
-            vm((rows, half), f32),
             vm((1, depth), f32),
             vm((1, half), f32),
-            vm((n - 1, 1, depth // n), f32),
+            vm((1, half), f32),
+            vm((nz - 1, 1, depth // n), f32),
             vm((1, depth), f32),
             vm((8, width), f32),
             dma((6,)),
-            dma((13,)),
-            dma((7,)),
+            dma((15,)),
+            dma((9,)),
             dma((3,)),
             dma((chunks,)),
             dma((chunks,)),
-            dma((2, 28)),
-            dma((2, 28)),
+            dma((2, 21)),
+            dma((2, 20)),
+            dma((2, 2, 2)),
             dma((tiles,)),
         ],
         compiler_params=pltpu.CompilerParams(

time: 95.7 us -> 93.3 us (0.975)
  Pallas kernels: 95 us -> 92.6 us
    pallas_call x1, Pallas kernels: 93.7 us -> 91.4 us  [shards(): pl.pallas_call(functools.partial(kernel, nz, ndp), out_shape=(vm((every,...]
where the time goes in v3:
time: 93.3 us
  Pallas kernels  92.6 us (99%)
    pallas_call x1, Pallas kernels, shards(): pl.pallas_call(functools.partial(kernel, nz, ndp), out_shape=(vm((every,...  91.4 us

profile of v3, /device:TPU:1, one launch (start us, length us, event | category | flops | bytes accessed | tf_op | source)
XLA Modules:
  0.0 93.3 jit_solution(17424906184230633114)
XLA Ops:
  0.6 91.4 %shard_map.93 = (bf16[512,640]{1,0:T(8,128)(2,1)S(1)}, f32[32,8192]{1,0:T(8,128)S(1)}, f32[1,8192]{1,0:T(1,128)S(1)}, f32[1,640]{1,0:T(1,128)S(1)}) custom-call(bf16[32,8192]{1,0:T(8,128)(2,1)} %tok_h.1, f32[8192]{0:T(1024)} %gain_h.1, bf16[8192,640]{1,0:T(8,128)(2,1)} %w_h.1, f32[640]{0:T(1024)} %bias_h.1, bf16[512,640]{1,0:T(8,128)(2,1)} %grad_h.1, ...), custom_call_target="tpu_custom_call" | custom-call | flops 10737418240 | bytes 10485760 | tf_op jit(solution)/shard_map/pallas_call | solution.py:473
  92.0 1.2 %shard_map.94 = (bf16[512,640]{1,0:T(8,128)(2,1)}, f32[32,8192]{1,0:T(8,128)}, f32[8192]{0:T(1024)}, f32[640]{0:T(1024)}) custom-call(bf16[512,640]{1,0:T(8,128)(2,1)S(1)} %get-tuple-element.8.qkv, f32[32,8192]{1,0:T(8,128)S(1)} %get-tuple-element.9.tg, f32[1,8192]{1,0:T(1,128)S(1)} %get-tuple-element.10.gg, f32[1,640]{1,0:T(1,128)S(1)} %get-tuple-element.11.bg), custom_call_target="tpu_custom_call" | custom-call | tf_op jit(solution)/shard_map/pallas_call | solution.py:529

commit v4 on v3

--- a/solution.py
+++ b/solution.py
@@ -38,10 +38,10 @@
 def kernel(
     nz, ndp,
     tok_h, gain_h, w_h, bias_h, grad_h, rope_h,
-    qkv, tg, gg_ref, bg_ref,
-    tok, gain, w, bias, grad, rope,
+    qkv, total_ng, tok, gain, factors, gg_ref, bg_ref,
+    w, bias, grad, rope,
     low, lowx, nx, held, part, run, rfin, acc, cx, qt, qx, ng, gtot, gx, gy, grecv, gres, bacc,
-    in_sem, send_sem, one_sem, low_r, wy_r, wx_r, ag_r, rs_r, end_r, c_r,
+    in_sem, send_sem, one_sem, low_r, wy_r, wx_r, ag_r, end_r, c_r,
 ):
     f32, bf16 = jnp.float32, jnp.bfloat16
     dp, mp = lax.axis_index("dp"), lax.axis_index("mp")
@@ -104,6 +104,13 @@
     def w_pass(a):
         ref = w.at[at((2 * a + odd) * WCHUNK, WCHUNK, WCHUNK), pair_cols]
         return remote(ref, ref, 1, wx_r.at[a], east if a % 2 == 0 else west)
+
+    def w_last():
+        i = 2 * chunks - 1 - odd
+        return remote(
+            w_h.at[at(core * half + i * WCHUNK, WCHUNK, WCHUNK), :],
+            w.at[at(i * WCHUNK, WCHUNK, WCHUNK), pair_cols], 0, wx_r.at[chunks - 1], pair,
+        )
 
     def w_come(k):
         ref = w.at[at((2 * k + 1 - odd) * WCHUNK, WCHUNK, WCHUNK), pair_cols]
@@ -176,6 +183,7 @@
     low_twin.start()
     for a in (2, 4, 6):
         w_send(a, pair).start()
+    w_last().start()
     nx_send.wait_recv()
     for q in range(4):
         for way in range(2):
@@ -186,6 +194,10 @@
         return at(k * CHUNK, CHUNK, CHUNK)
 
     def backward(k):
+        @pl.when(k == chunks - 1)
+        def _():
+            w_send(chunks - 1, far).wait_recv()
+
         w_come(k).wait_recv()
         part[:, cols(k)] = lax.dot_general(
             low[...], w[cols(k), :], (((1,), (1,)), ((), ())), preferred_element_type=f32
@@ -194,7 +206,7 @@
     def rs(way, j, k):
         place = j * 8 + jnp.where(j < 2, k, k // 2)
         return remote(
-            run.at[way, j, :, cols(k)], run.at[way, j + 1, :, cols(k)], 6, rs_r.at[way, place], along[way]
+            run.at[way, j, :, cols(k)], run.at[way, j + 1, :, cols(k)], 6, ag_r.at[way, place], along[way]
         )
 
     def rs_end(way, j, k, d):
@@ -300,8 +312,9 @@
             def _():
                 q_send(h - heads).start()
 
-    passes = (3, 8, 10, 13, 15, 18, 20, 23)
-    early = (11, 16, 18, 21, 23)
+    passes = (4, 9, 11, 14, 16, 19, 21)
+    early = (12, 17, 18, 22, 23)
+    ahead = 4
 
     @pl.loop(0, 24)
     def _(i):
@@ -312,6 +325,11 @@
                 ag(way, j - 1, e).wait_recv()
                 ag(way, j, e).start()
 
+        @pl.when(i >= 24 - ahead)
+        def _():
+            for way in range(2):
+                rs_step(way, 0, i - (24 - ahead), True)
+
         for a, step in enumerate(passes):
             @pl.when(i == step)
             def _():
@@ -337,9 +355,11 @@
         def _():
             backward(k)
 
-    @pl.loop(0, chunks)
-    def _(k):
-        @pl.when(k >= len(early))
+    @pl.loop(ahead, chunks)
+    def _(m):
+        k = jnp.where(m < chunks - 2, m, 2 * chunks - 3 - m)
+
+        @pl.when(m >= len(early))
         def _():
             backward(k)
 
@@ -418,12 +438,10 @@
     for q in range(2 * chunks):
         ks = slice(q * CHUNK, (q + 1) * CHUNK)
         v = ng[:, ks] + rfin[q % 2, :, ks].astype(f32)
-        ng[:, ks] = v
+        total_ng[:, ks] = v
         inner = inner + jnp.sum(v * tok[:, ks].astype(f32) * gain[:, ks], axis=1, keepdims=True)
-    weight = scale * scale * scale * (inner / depth)
-    for q in range(8):
-        ks = slice(q * quarter, (q + 1) * quarter)
-        tg[:, ks] = scale * gain[:, ks] * ng[:, ks] - tok[:, ks].astype(f32) * weight
+    factors[0] = jnp.broadcast_to(scale, factors.shape[1:])
+    factors[1] = jnp.broadcast_to(scale * scale * scale * (inner / depth), factors.shape[1:])
 
     g3_send.wait_recv()
     gg_ref[...] = gres[...]
@@ -431,8 +449,8 @@
     def sent(ref, send):
         remote(ref, ref, send, one_sem.at[0], twin).wait_send()
 
-    sent(w_h.at[pl.ds(0, half // 2), :], 0)
-    sent(w_h.at[pl.ds(0, half // 2), :], 1)
+    sent(w_h.at[pl.ds(0, (chunks + 1) * WCHUNK), :], 0)
+    sent(w_h.at[pl.ds(0, (chunks - 1) * WCHUNK), :], 1)
     sent(nx, 2)
     moved = held.at[pl.ds(0, 7 * 2 * rows), :]
     sent(moved, 3)
@@ -449,11 +467,22 @@
     g3_send.wait_send()
 
 
-def finish(qkv, tg, gg, bg, qkv_h, tg_h, gg_h, bg_h, sem):
-    moves = ((qkv, qkv_h), (tg, tg_h), (gg.at[0], gg_h), (bg.at[0], bg_h))
-    copies = [pltpu.make_async_copy(src, dst, sem.at[i]) for i, (src, dst) in enumerate(moves)]
+def finish(qkv, ng, tok, gain, factors, gg, bg, qkv_h, tg_h, gg_h, bg_h, tg, sem):
+    parts = sem.shape[0] - 3
+    piece = tok.shape[1] // parts
+    copies = [
+        pltpu.make_async_copy(src, dst, sem.at[i])
+        for i, (src, dst) in enumerate(((qkv, qkv_h), (gg.at[0], gg_h), (bg.at[0], bg_h)))
+    ]
     for c in copies:
         c.start()
+    scale, weight = factors[0, :, :1], factors[1, :, :1]
+    for q in range(parts):
+        ks = slice(q * piece, (q + 1) * piece)
+        tg[:, ks] = scale * gain[:, ks] * ng[:, ks] - tok[:, ks].astype(jnp.float32) * weight
+        c = pltpu.make_async_copy(tg.at[:, ks], tg_h.at[:, ks], sem.at[3 + q])
+        c.start()
+        copies.append(c)
     for c in copies:
         c.wait()
 
@@ -475,14 +504,15 @@
         out_shape=(
             vm((every, width), bf16),
             vm((rows, depth), f32),
+            vm((rows, depth), bf16),
+            vm((1, depth), f32),
+            vm((2, rows, HEAD_DIM), f32),
             vm((1, depth), f32),
             vm((1, width), f32),
         ),
         in_specs=[hbm] * 6,
-        out_specs=[vmem] * 4,
+        out_specs=[vmem] * 7,
         scratch_shapes=[
-            vm((rows, depth), bf16),
-            vm((1, depth), f32),
             vm((half, 2 * width), bf16),
             vm((1, 2 * width), f32),
             vm((every, width), bf16),
@@ -512,7 +542,6 @@
             dma((chunks,)),
             dma((chunks,)),
             dma((2, 21)),
-            dma((2, 20)),
             dma((2, 2, 2)),
             dma((tiles,)),
         ],
@@ -534,10 +563,10 @@
             jax.ShapeDtypeStruct((depth,), f32),
             jax.ShapeDtypeStruct((width,), f32),
         ),
-        in_specs=[vmem] * 4,
+        in_specs=[vmem] * 7,
         out_specs=[hbm] * 4,
-        scratch_shapes=[dma((4,))],
-        compiler_params=pltpu.CompilerParams(vmem_limit_bytes=1 << 20),
+        scratch_shapes=[vm((rows, depth), f32), dma((7,))],
+        compiler_params=pltpu.CompilerParams(vmem_limit_bytes=1 << 21),
     )(*results)
 
 

time: 93.3 us -> 92.9 us (level)
  no operation moved by 1% of the time
where the time goes in v4:
time: 92.9 us; the launch traced here: 92.8 us
  Pallas kernels  92.2 us (99%)
    pallas_call x1, Pallas kernels, shards(): pl.pallas_call(functools.partial(kernel, nz, ndp), out_shape=(vm((every,...  90.9 us

profile of v4, /device:TPU:1, one launch (start us, length us, event | category | flops | bytes accessed | tf_op | source)
XLA Modules:
  0.0 92.8 jit_solution(15267005339446524493)
XLA Ops:
  0.6 90.9 %shard_map.93 = (bf16[512,640]{1,0:T(8,128)(2,1)S(1)}, f32[32,8192]{1,0:T(8,128)S(1)}, bf16[32,8192]{1,0:T(8,128)(2,1)S(1)}, f32[1,8192]{1,0:T(1,128)S(1)}, f32[...) custom-call(bf16[32,8192]{1,0:T(8,128)(2,1)} %tok_h.1, f32[8192]{0:T(1024)} %gain_h.1, ...), custom_call_target="tpu_custom_call" | custom-call | flops 10737418240 | bytes 10485760 | tf_op jit(solution)/shard_map/pallas_call | solution.py:502
  91.5 1.3 %shard_map.94 = (bf16[512,640]{1,0:T(8,128)(2,1)}, f32[32,8192]{1,0:T(8,128)}, f32[8192]{0:T(1024)}, f32[640]{0:T(1024)}) custom-call(bf16[512,640]{1,0:T(8,128)(2,1)S(1)} %get-tuple-element.11.qkv, f32[32,8192]{1,0:T(8,128)S(1)} %get-tuple-element.12.ng, bf16[32,8192]{1,0:T(8,128)(2,1)S(1)} %get-tuple-element.13.tok, f32[1,8192]{1,0:T(1,128)S(1)} %get-tuple-element.14.gain, ...), custom_call_target="tpu_custom_call" | custom-call | tf_op jit(solution)/shard_map/pallas_call | solution.py:558

commit v5 on v4

--- a/solution.py
+++ b/solution.py
@@ -40,7 +40,7 @@
     tok_h, gain_h, w_h, bias_h, grad_h, rope_h,
     qkv, total_ng, tok, gain, factors, gg_ref, bg_ref,
     w, bias, grad, rope,
-    low, lowx, nx, held, part, run, rfin, acc, cx, qt, qx, ng, gtot, gx, gy, grecv, gres, bacc,
+    low, lowx, nx, held, part, run, rfin, acc, cx, qt, qx, ng, gtot, gx, gy, gstage, gsend, grecv, gdone, gres, bacc,
     in_sem, send_sem, one_sem, low_r, wy_r, wx_r, ag_r, end_r, c_r,
 ):
     f32, bf16 = jnp.float32, jnp.bfloat16
@@ -213,7 +213,7 @@
         return remote(
             run.at[way, j, pl.ds(d * rows, rows), cols(k)],
             rfin.at[way, :, at(core * half + k * CHUNK, CHUNK, CHUNK)],
-            6, end_r.at[way, core, j - 2], dict(along[way], dp=dp - core + d),
+            6, end_r.at[way, core, jnp.where(j < 3, 0, jnp.where(k < chunks - 2, 1, 2))], dict(along[way], dp=dp - core + d),
         )
 
     def hops(way, k):
@@ -249,9 +249,10 @@
     )
 
     def ended(group):
+        count = (chunks // 2, chunks // 2 - 1, 1)[group]
         for way in range(2):
             for side in range(2):
-                ref = rfin.at[way, :, pl.ds(0, half // 2)]
+                ref = rfin.at[way, :, pl.ds(0, count * CHUNK)]
                 remote(ref, ref, 6, end_r.at[way, side, group], up).wait_recv()
 
     def gain_share(k):
@@ -265,20 +266,21 @@
     column_half = at(yl * half, half, half)
     g3_send = remote(gres.at[:, column_half], gres.at[:, column_half], 14, one_sem.at[8], pair)
 
-    def slab_of(i):
-        return at(yl * half + i * slab, slab, slab)
+    lines = slab // HEAD_DIM
+
+    def line_of(zz, i):
+        return at(yl * half + zz * slab + i * HEAD_DIM, HEAD_DIM, HEAD_DIM)
 
     def g1(k):
         to = lax.rem(z + k, nz)
-        return remote(gtot.at[:, slab_of(to)], grecv.at[k - 1], 9, one_sem.at[4], {"mp": 2 * to + yl})
+        return remote(gsend.at[to], grecv.at[k - 1], 9, one_sem.at[4], {"mp": 2 * to + yl})
 
     def g2(k):
         to = lax.rem(z + k, nz)
-        return remote(gres.at[:, slab_of(z)], gres.at[:, slab_of(z)], 10, one_sem.at[5], {"mp": 2 * to + yl})
+        return remote(gdone.at[z], gdone.at[z], 10, one_sem.at[5], {"mp": 2 * to + yl})
 
     g1_all = remote(grecv, grecv, 9, one_sem.at[4], up)
-    g2_ref = gres.at[:, pl.ds(0, (nz - 1) * slab)]
-    g2_all = remote(g2_ref, g2_ref, 10, one_sem.at[5], up)
+    g2_all = remote(grecv, grecv, 10, one_sem.at[5], up)
 
     def tile(t):
         return at(t * TILE_N, TILE_N, TILE_N)
@@ -405,16 +407,20 @@
         def _():
             gy_send.wait_recv()
             gtot[:, column_half] += gy[...]
+            for zz in range(nz):
+                for i in range(lines):
+                    gstage[zz, i:i + 1, :] = gtot[:, line_of(zz, i)]
+            gsend[...] = gstage[...].astype(bf16)
             for k in range(1, nz):
                 g1(k).start()
 
         @pl.when(m == 13)
         def _():
             g1_all.wait_recv()
-            share = gtot[:, slab_of(z)]
+            share = gstage[z]
             for k in range(1, nz):
-                share = share + grecv[k - 1]
-            gres[:, slab_of(z)] = share
+                share = share + grecv[k - 1].astype(f32)
+            gdone[z] = share.astype(bf16)
             for k in range(1, nz):
                 g2(k).start()
 
@@ -427,19 +433,26 @@
                 qkv[at((2 * b + 1 - yl) * rows, rows, rows), :] = qx[there, :]
 
     g2_all.wait_recv()
+    gstage[...] = gdone[...].astype(f32)
+    for zz in range(nz):
+        for i in range(lines):
+            gres[:, line_of(zz, i)] = gstage[zz, i:i + 1, :]
     g3_send.start()
     swap.wait_recv()
     ended(0)
     for q in range(2 * chunks):
         ks = slice(q * CHUNK, (q + 1) * CHUNK)
         ng[:, ks] += rfin[1 - q % 2, :, ks].astype(f32)
-    ended(1)
     inner = jnp.zeros((rows, 1), f32)
-    for q in range(2 * chunks):
-        ks = slice(q * CHUNK, (q + 1) * CHUNK)
-        v = ng[:, ks] + rfin[q % 2, :, ks].astype(f32)
-        total_ng[:, ks] = v
-        inner = inner + jnp.sum(v * tok[:, ks].astype(f32) * gain[:, ks], axis=1, keepdims=True)
+    for group, ks_in in ((1, range(chunks - 2)), (2, range(chunks - 2, chunks))):
+        ended(group)
+        for side in range(2):
+            for k in ks_in:
+                q = side * chunks + k
+                ks = slice(q * CHUNK, (q + 1) * CHUNK)
+                v = ng[:, ks] + rfin[k % 2, :, ks].astype(f32)
+                total_ng[:, ks] = v
+                inner = inner + jnp.sum(v * tok[:, ks].astype(f32) * gain[:, ks], axis=1, keepdims=True)
     factors[0] = jnp.broadcast_to(scale, factors.shape[1:])
     factors[1] = jnp.broadcast_to(scale * scale * scale * (inner / depth), factors.shape[1:])
 
@@ -493,6 +506,7 @@
     rope = rope_tables(every, rows, SEQ_LEN // n)
     bf16, f32 = jnp.bfloat16, jnp.float32
     half, col, nz = depth // 2, every // 2, n // 2
+    slab = half // nz
     chunks = half // CHUNK
     tiles = 2 * width // TILE_N
     dma = pltpu.SemaphoreType.DMA
@@ -532,7 +546,10 @@
             vm((1, depth), f32),
             vm((1, half), f32),
             vm((1, half), f32),
-            vm((nz - 1, 1, depth // n), f32),
+            vm((nz, slab // HEAD_DIM, HEAD_DIM), f32),
+            vm((nz, slab // HEAD_DIM, HEAD_DIM), bf16),
+            vm((nz - 1, slab // HEAD_DIM, HEAD_DIM), bf16),
+            vm((nz, slab // HEAD_DIM, HEAD_DIM), bf16),
             vm((1, depth), f32),
             vm((8, width), f32),
             dma((6,)),
@@ -542,7 +559,7 @@
             dma((chunks,)),
             dma((chunks,)),
             dma((2, 21)),
-            dma((2, 2, 2)),
+            dma((2, 2, 3)),
             dma((tiles,)),
         ],
         compiler_params=pltpu.CompilerParams(

time: 92.9 us -> 92.4 us (level)
  no operation moved by 1% of the time
where the time goes in v5:
time: 92.4 us; the launch traced here: 92.3 us
  Pallas kernels  91.7 us (99%)
    pallas_call x1, Pallas kernels, shards(): pl.pallas_call(functools.partial(kernel, nz, ndp), out_shape=(vm((every,...  90.4 us

profile of v5, /device:TPU:1, one launch (start us, length us, event | category | flops | bytes accessed | tf_op | source)
XLA Modules:
  0.0 92.3 jit_solution(11903810014020103431)
XLA Ops:
  0.6 90.4 %shard_map.93 = (bf16[512,640]{1,0:T(8,128)(2,1)S(1)}, f32[32,8192]{1,0:T(8,128)S(1)}, bf16[32,8192]{1,0:T(8,128)(2,1)S(1)}, f32[1,8192]{1,0:T(1,128)S(1)}, f32[...) custom-call(bf16[32,8192]{1,0:T(8,128)(2,1)} %tok_h.1, f32[8192]{0:T(1024)} %gain_h.1, ...), custom_call_target="tpu_custom_call" | custom-call | flops 10737418240 | bytes 10485760 | tf_op jit(solution)/shard_map/pallas_call | solution.py:516
  91.1 1.3 %shard_map.94 = (bf16[512,640]{1,0:T(8,128)(2,1)}, f32[32,8192]{1,0:T(8,128)}, f32[8192]{0:T(1024)}, f32[640]{0:T(1024)}) custom-call(bf16[512,640]{1,0:T(8,128)(2,1)S(1)} %get-tuple-element.11.qkv, f32[32,8192]{1,0:T(8,128)S(1)} %get-tuple-element.12.ng, bf16[32,8192]{1,0:T(8,128)(2,1)S(1)} %get-tuple-element.13.tok, f32[1,8192]{1,0:T(1,128)S(1)} %get-tuple-element.14.gain, ...), custom_call_target="tpu_custom_call" | custom-call | tf_op jit(solution)/shard_map/pallas_call | solution.py:575

commit v6 on v5

--- a/solution.py
+++ b/solution.py
@@ -41,7 +41,7 @@
     qkv, total_ng, tok, gain, factors, gg_ref, bg_ref,
     w, bias, grad, rope,
     low, lowx, nx, held, part, run, rfin, acc, cx, qt, qx, ng, gtot, gx, gy, gstage, gsend, grecv, gdone, gres, bacc,
-    in_sem, send_sem, one_sem, low_r, wy_r, wx_r, ag_r, end_r, c_r,
+    in_sem, send_sem, one_sem, low_r, wy_r, wx_r, ag_r, end_r, turn_r, c_r,
 ):
     f32, bf16 = jnp.float32, jnp.bfloat16
     dp, mp = lax.axis_index("dp"), lax.axis_index("mp")
@@ -219,20 +219,57 @@
     def hops(way, k):
         return jnp.where(lax.rem(k, 2) == way, 4, 3)
 
-    def rs_step(way, j, k, first):
+    turning = (nz - 1, 1)
+
+    def turned(way):
+        return remote(
+            run.at[way, 0, :, cols(way)], run.at[1 - way, 0, :, cols(way)], 6, turn_r.at[way], along[1 - way]
+        )
+
+    def rs_term(way, j, k, more):
         left = hops(way, k) - j
         t = lax.rem(z + (left if way == 0 else nz - left), nz)
-        if not first:
-            rs(way, j - 1, k).wait_recv()
         for d in range(2):
             ds = pl.ds(d * rows, rows)
             v = part[at(d * col + t * rows, rows, rows), cols(k)]
-            if not first:
+            if more:
                 v = v + run[way, j, ds, cols(k)].astype(f32)
             run[way, j, ds, cols(k)] = v.astype(bf16)
-        if first:
-            rs(way, j, k).start()
-            return
+
+    def rs_turn(way):
+        @pl.when(z == turning[way])
+        def _():
+            rs_term(way, 0, way, False)
+            turned(way).start()
+
+    def rs_first(way, k):
+        joins = (k == 1 - way) & (z == (2, nz - 2)[way])
+
+        @pl.when((k != way) | (z != turning[way]))
+        def _():
+            @pl.when(joins)
+            def _():
+                turned(1 - way).wait_recv()
+                rs_term(way, 0, k, True)
+
+            @pl.when(jnp.logical_not(joins))
+            def _():
+                rs_term(way, 0, k, False)
+
+            rs(way, 0, k).start()
+
+    def rs_step(way, j, k):
+        left = hops(way, k) - j
+        starts = (j == 1) & (k == way) & (z == 0)
+
+        @pl.when(starts)
+        def _():
+            rs_term(way, j, k, False)
+
+        @pl.when(jnp.logical_not(starts))
+        def _():
+            rs(way, j - 1, k).wait_recv()
+            rs_term(way, j, k, True)
 
         @pl.when(left > 1)
         def _():
@@ -316,7 +353,7 @@
 
     passes = (4, 9, 11, 14, 16, 19, 21)
     early = (12, 17, 18, 22, 23)
-    ahead = 4
+    ahead = 3
 
     @pl.loop(0, 24)
     def _(i):
@@ -329,8 +366,17 @@
 
         @pl.when(i >= 24 - ahead)
         def _():
+            k = i - (24 - ahead)
             for way in range(2):
-                rs_step(way, 0, i - (24 - ahead), True)
+                rs_first(way, jnp.where(k < 1, k, k + 1))
+
+        @pl.when(i == 13)
+        def _():
+            rs_turn(0)
+
+        @pl.when(i == 18)
+        def _():
+            rs_turn(1)
 
         for a, step in enumerate(passes):
             @pl.when(i == step)
@@ -359,14 +405,14 @@
 
     @pl.loop(ahead, chunks)
     def _(m):
-        k = jnp.where(m < chunks - 2, m, 2 * chunks - 3 - m)
+        k = jnp.where(m == ahead, 1, jnp.where(m < chunks - 2, m, 2 * chunks - 3 - m))
 
         @pl.when(m >= len(early))
         def _():
             backward(k)
 
         for way in range(2):
-            rs_step(way, 0, k, True)
+            rs_first(way, k)
 
     swap.start()
     for q in range(4):
@@ -388,7 +434,7 @@
     def _(m):
         j, q = 1 + m // 8, lax.rem(m, 8)
         for way in range(2):
-            rs_step(way, j, jnp.where(j < 3, q, 2 * q + way), False)
+            rs_step(way, j, jnp.where(j < 3, q, 2 * q + way))
 
         @pl.when((m >= 2) & (m < 7))
         def _():
@@ -560,6 +606,7 @@
             dma((chunks,)),
             dma((2, 21)),
             dma((2, 2, 3)),
+            dma((2,)),
             dma((tiles,)),
         ],
         compiler_params=pltpu.CompilerParams(

time: 92.4 us -> 91 us (0.985)
  Pallas kernels: 91.7 us -> 90.3 us
    pallas_call x1, Pallas kernels: 90.4 us -> 89 us  [shards(): pl.pallas_call(functools.partial(kernel, nz, ndp), out_shape=(vm((every,...]
where the time goes in v6:
time: 91 us; the launch traced here: 90.9 us
  Pallas kernels  90.3 us (99%)
    pallas_call x1, Pallas kernels, shards(): pl.pallas_call(functools.partial(kernel, nz, ndp), out_shape=(vm((every,...  89 us

profile of v6, /device:TPU:1, one launch (start us, length us, event | category | flops | bytes accessed | tf_op | source)
XLA Modules:
  0.0 90.9 jit_solution(2914864902482392763)
XLA Ops:
  0.6 89.0 %shard_map.93 = (bf16[512,640]{1,0:T(8,128)(2,1)S(1)}, f32[32,8192]{1,0:T(8,128)S(1)}, bf16[32,8192]{1,0:T(8,128)(2,1)S(1)}, f32[1,8192]{1,0:T(1,128)S(1)}, f32[...) custom-call(bf16[32,8192]{1,0:T(8,128)(2,1)} %tok_h.1, f32[8192]{0:T(1024)} %gain_h.1, ...), custom_call_target="tpu_custom_call" | custom-call | flops 10737418240 | bytes 10485760 | tf_op jit(solution)/shard_map/pallas_call | solution.py:562
  89.7 1.3 %shard_map.94 = (bf16[512,640]{1,0:T(8,128)(2,1)}, f32[32,8192]{1,0:T(8,128)}, f32[8192]{0:T(1024)}, f32[640]{0:T(1024)}) custom-call(bf16[512,640]{1,0:T(8,128)(2,1)S(1)} %get-tuple-element.11.qkv, f32[32,8192]{1,0:T(8,128)S(1)} %get-tuple-element.12.ng, bf16[32,8192]{1,0:T(8,128)(2,1)S(1)} %get-tuple-element.13.tok, f32[1,8192]{1,0:T(1,128)S(1)} %get-tuple-element.14.gain, ...), custom_call_target="tpu_custom_call" | custom-call | tf_op jit(solution)/shard_map/pallas_call | solution.py:622

commit v7 on v6

--- a/solution.py
+++ b/solution.py
@@ -15,6 +15,7 @@
 CHUNK = 512
 WCHUNK = 256
 TILE_N = 256
+TURNED = 2
 
 
 def rope_tables(rows, tok_dev, stride):
@@ -221,9 +222,9 @@
 
     turning = (nz - 1, 1)
 
-    def turned(way):
+    def turned(way, k):
         return remote(
-            run.at[way, 0, :, cols(way)], run.at[1 - way, 0, :, cols(way)], 6, turn_r.at[way], along[1 - way]
+            run.at[way, 0, :, cols(k)], run.at[1 - way, 0, :, cols(k)], 6, turn_r.at[way, k], along[1 - way]
         )
 
     def rs_term(way, j, k, more):
@@ -236,20 +237,21 @@
                 v = v + run[way, j, ds, cols(k)].astype(f32)
             run[way, j, ds, cols(k)] = v.astype(bf16)
 
-    def rs_turn(way):
-        @pl.when(z == turning[way])
-        def _():
-            rs_term(way, 0, way, False)
-            turned(way).start()
+    def rs_turn(k):
+        for way in range(2):
+            @pl.when(z == turning[way])
+            def _():
+                rs_term(way, 0, k, False)
+                turned(way, k).start()
 
     def rs_first(way, k):
-        joins = (k == 1 - way) & (z == (2, nz - 2)[way])
-
-        @pl.when((k != way) | (z != turning[way]))
+        joins = (k < TURNED) & (z == (2, nz - 2)[way])
+
+        @pl.when((k >= TURNED) | (z != turning[way]))
         def _():
             @pl.when(joins)
             def _():
-                turned(1 - way).wait_recv()
+                turned(1 - way, jnp.where(k < TURNED, k, 0)).wait_recv()
                 rs_term(way, 0, k, True)
 
             @pl.when(jnp.logical_not(joins))
@@ -260,7 +262,7 @@
 
     def rs_step(way, j, k):
         left = hops(way, k) - j
-        starts = (j == 1) & (k == way) & (z == 0)
+        starts = (j == 1) & (k < TURNED) & (z == 0)
 
         @pl.when(starts)
         def _():
@@ -606,7 +608,7 @@
             dma((chunks,)),
             dma((2, 21)),
             dma((2, 2, 3)),
-            dma((2,)),
+            dma((2, TURNED)),
             dma((tiles,)),
         ],
         compiler_params=pltpu.CompilerParams(

time: 91 us -> 89.6 us (0.985)
  Pallas kernels: 90.3 us -> 88.9 us
    pallas_call x1, Pallas kernels: 89 us -> 87.7 us  [shards(): pl.pallas_call(functools.partial(kernel, nz, ndp), out_shape=(vm((every,...]
where the time goes in v7:
time: 89.6 us; the launch traced here: 89.5 us
  Pallas kernels  88.9 us (99%)
    pallas_call x1, Pallas kernels, shards(): pl.pallas_call(functools.partial(kernel, nz, ndp), out_shape=(vm((every,...  87.7 us

profile of v7, /device:TPU:1, one launch (start us, length us, event | category | flops | bytes accessed | tf_op | source)
XLA Modules:
  0.0 89.5 jit_solution(6034344112247327463)
XLA Ops:
  0.6 87.7 %shard_map.93 = (bf16[512,640]{1,0:T(8,128)(2,1)S(1)}, f32[32,8192]{1,0:T(8,128)S(1)}, bf16[32,8192]{1,0:T(8,128)(2,1)S(1)}, f32[1,8192]{1,0:T(1,128)S(1)}, f32[...) custom-call(bf16[32,8192]{1,0:T(8,128)(2,1)} %tok_h.1, f32[8192]{0:T(1024)} %gain_h.1, ...), custom_call_target="tpu_custom_call" | custom-call | flops 10737418240 | bytes 10485760 | tf_op jit(solution)/shard_map/pallas_call | solution.py:564
  88.3 1.3 %shard_map.94 = (bf16[512,640]{1,0:T(8,128)(2,1)}, f32[32,8192]{1,0:T(8,128)}, f32[8192]{0:T(1024)}, f32[640]{0:T(1024)}) custom-call(bf16[512,640]{1,0:T(8,128)(2,1)S(1)} %get-tuple-element.11.qkv, f32[32,8192]{1,0:T(8,128)S(1)} %get-tuple-element.12.ng, bf16[32,8192]{1,0:T(8,128)(2,1)S(1)} %get-tuple-element.13.tok, f32[1,8192]{1,0:T(1,128)S(1)} %get-tuple-element.14.gain, ...), custom_call_target="tpu_custom_call" | custom-call | tf_op jit(solution)/shard_map/pallas_call | solution.py:624

commit v8 on v7

--- a/solution.py
+++ b/solution.py
@@ -72,20 +72,21 @@
     west = {"dp": row_of_x + lax.rem(x + nx_chips - 1, nx_chips) * 2 + core}
     along = (up, down)
 
+    loads = [
+        pltpu.make_async_copy(src, dst, in_sem.at[i])
+        for i, (src, dst) in enumerate((
+            (tok_h, tok), (gain_h, gain.at[0]), (grad_h, grad), (rope_h, rope),
+            (bias_h, bias.at[0, pl.ds(0, width)]),
+            (w_h.at[at(core * half, half, half), :], w.at[:, pl.ds(0, width)]),
+        ))
+    ]
+    loads[0].start()
+    loads[1].start()
+
     barrier = pltpu.get_barrier_semaphore()
     peers = (up, down, pair, far, twin, east, west)
     for there in peers:
         pl.semaphore_signal(barrier, inc=1, device_id=there, device_id_type=MESH)
-
-    loads = []
-    for i, (src, dst) in enumerate((
-        (tok_h, tok), (gain_h, gain.at[0]), (grad_h, grad), (rope_h, rope),
-        (bias_h, bias.at[0, pl.ds(0, width)]),
-        (w_h.at[at(core * half, half, half), :], w.at[:, pl.ds(0, width)]),
-    )):
-        c = pltpu.make_async_copy(src, dst, in_sem.at[i])
-        c.start()
-        loads.append(c)
 
     def remote(src, dst, send, recv, there):
         return pltpu.make_async_remote_copy(
@@ -104,7 +105,7 @@
 
     def w_pass(a):
         ref = w.at[at((2 * a + odd) * WCHUNK, WCHUNK, WCHUNK), pair_cols]
-        return remote(ref, ref, 1, wx_r.at[a], east if a % 2 == 0 else west)
+        return remote(ref, ref, 0, wx_r.at[a], east if a % 2 == 0 else west)
 
     def w_last():
         i = 2 * chunks - 1 - odd
@@ -115,12 +116,12 @@
 
     def w_come(k):
         ref = w.at[at((2 * k + 1 - odd) * WCHUNK, WCHUNK, WCHUNK), pair_cols]
-        return remote(ref, ref, 1, wx_r.at[k], east)
+        return remote(ref, ref, 0, wx_r.at[k], east)
 
     mine = at(core * col, col, col)
     other = at((1 - core) * col, col, col)
     home = at(core * col + z * rows, rows, rows)
-    nx_send = remote(nx, held.at[home, :], 2, one_sem.at[0], twin)
+    nx_send = remote(nx, held.at[home, :], 1, one_sem.at[0], twin)
 
     def ag(way, j, e):
         d = lax.rem(core + e // 4, 2)
@@ -128,10 +129,12 @@
         ref = held.at[at(d * col + b * rows, rows, rows), at(lax.rem(e, 4) * quarter, quarter, quarter)]
         on = jnp.where(lax.rem(e, 2) == way, 16 + e // 2, 20)
         place = jnp.where(j < 2, j * 8 + e, jnp.where(j == 2, on, 20))
-        return remote(ref, ref, 3, ag_r.at[way, place], along[way])
+        return remote(ref, ref, 1, ag_r.at[way, place], along[way])
 
     loads[0].wait()
     loads[1].wait()
+    for l in loads[2:]:
+        l.start()
     total = jnp.zeros((rows, 1), f32)
     for q in range(8):
         v = tok[:, q * quarter:(q + 1) * quarter].astype(f32)
@@ -143,12 +146,12 @@
 
     for q in range(4):
         held[home, q * quarter:(q + 1) * quarter] = normed(at(core * half + q * quarter, quarter, quarter))
-    for q in range(4):
-        nx[:, q * quarter:(q + 1) * quarter] = normed(at((1 - core) * half + q * quarter, quarter, quarter))
     pl.semaphore_wait(barrier, len(peers))
     for q in range(4):
         for way in range(2):
             ag(way, 0, q).start()
+    for q in range(4):
+        nx[:, q * quarter:(q + 1) * quarter] = normed(at((1 - core) * half + q * quarter, quarter, quarter))
     nx_send.start()
     bias_send = remote(bias_h, bias.at[0, pair_cols], 4, one_sem.at[1], pair)
     bias_send.start()
@@ -177,9 +180,9 @@
                 else:
                     lowx[there, hs] = v.astype(bf16)
 
-    low_pair = remote(lowx, low.at[mine, pair_cols], 5, low_r.at[0], pair)
-    low_twin = remote(low.at[mine, own_cols], low.at[mine, own_cols], 5, low_r.at[1], twin)
-    low_fwd = remote(low.at[mine, pair_cols], low.at[mine, pair_cols], 5, low_r.at[2], twin)
+    low_pair = remote(lowx, low.at[mine, pair_cols], 0, low_r.at[0], pair)
+    low_twin = remote(low.at[mine, own_cols], low.at[mine, own_cols], 0, low_r.at[1], twin)
+    low_fwd = remote(low.at[mine, pair_cols], low.at[mine, pair_cols], 0, low_r.at[2], twin)
     low_pair.start()
     low_twin.start()
     for a in (2, 4, 6):
@@ -207,14 +210,14 @@
     def rs(way, j, k):
         place = j * 8 + jnp.where(j < 2, k, k // 2)
         return remote(
-            run.at[way, j, :, cols(k)], run.at[way, j + 1, :, cols(k)], 6, ag_r.at[way, place], along[way]
+            run.at[way, j, :, cols(k)], run.at[way, j + 1, :, cols(k)], 1, ag_r.at[way, place], along[way]
         )
 
     def rs_end(way, j, k, d):
         return remote(
             run.at[way, j, pl.ds(d * rows, rows), cols(k)],
             rfin.at[way, :, at(core * half + k * CHUNK, CHUNK, CHUNK)],
-            6, end_r.at[way, core, jnp.where(j < 3, 0, jnp.where(k < chunks - 2, 1, 2))], dict(along[way], dp=dp - core + d),
+            1, end_r.at[way, core, jnp.where(j < 3, 0, jnp.where(k < chunks - 2, 1, 2))], dict(along[way], dp=dp - core + d),
         )
 
     def hops(way, k):
@@ -224,7 +227,7 @@
 
     def turned(way, k):
         return remote(
-            run.at[way, 0, :, cols(k)], run.at[1 - way, 0, :, cols(k)], 6, turn_r.at[way, k], along[1 - way]
+            run.at[way, 0, :, cols(k)], run.at[1 - way, 0, :, cols(k)], 1, turn_r.at[way, k], along[1 - way]
         )
 
     def rs_term(way, j, k, more):
@@ -284,7 +287,7 @@
 
     own_half = at(core * half, half, half)
     swap = remote(
-        part.at[at((1 - core) * col + z * rows, rows, rows), :], ng.at[:, own_half], 7, one_sem.at[2], twin
+        part.at[at((1 - core) * col + z * rows, rows, rows), :], ng.at[:, own_half], 1, one_sem.at[2], twin
     )
 
     def ended(group):
@@ -292,7 +295,7 @@
         for way in range(2):
             for side in range(2):
                 ref = rfin.at[way, :, pl.ds(0, count * CHUNK)]
-                remote(ref, ref, 6, end_r.at[way, side, group], up).wait_recv()
+                remote(ref, ref, 1, end_r.at[way, side, group], up).wait_recv()
 
     def gain_share(k):
         full = at(core * half + k * CHUNK, CHUNK, CHUNK)
@@ -300,10 +303,10 @@
             share = jnp.sum(part[ds, cols(k)] * held[ds, cols(k)].astype(f32), axis=0, keepdims=True)
             to[:, ks] = share / gain[:, full]
 
-    gx_send = remote(gx, gtot.at[:, own_half], 8, one_sem.at[3], twin)
-    gy_send = remote(gtot.at[:, at((1 - yl) * half, half, half)], gy, 13, one_sem.at[7], pair)
+    gx_send = remote(gx, gtot.at[:, own_half], 3, one_sem.at[3], twin)
+    gy_send = remote(gtot.at[:, at((1 - yl) * half, half, half)], gy, 3, one_sem.at[7], pair)
     column_half = at(yl * half, half, half)
-    g3_send = remote(gres.at[:, column_half], gres.at[:, column_half], 14, one_sem.at[8], pair)
+    g3_send = remote(gres.at[:, column_half], gres.at[:, column_half], 7, one_sem.at[8], pair)
 
     lines = slab // HEAD_DIM
 
@@ -312,20 +315,20 @@
 
     def g1(k):
         to = lax.rem(z + k, nz)
-        return remote(gsend.at[to], grecv.at[k - 1], 9, one_sem.at[4], {"mp": 2 * to + yl})
+        return remote(gsend.at[to], grecv.at[k - 1], 5, one_sem.at[4], {"mp": 2 * to + yl})
 
     def g2(k):
         to = lax.rem(z + k, nz)
-        return remote(gdone.at[z], gdone.at[z], 10, one_sem.at[5], {"mp": 2 * to + yl})
-
-    g1_all = remote(grecv, grecv, 9, one_sem.at[4], up)
-    g2_all = remote(grecv, grecv, 10, one_sem.at[5], up)
+        return remote(gdone.at[z], gdone.at[z], 6, one_sem.at[5], {"mp": 2 * to + yl})
+
+    g1_all = remote(grecv, grecv, 5, one_sem.at[4], up)
+    g2_all = remote(grecv, grecv, 6, one_sem.at[5], up)
 
     def tile(t):
         return at(t * TILE_N, TILE_N, TILE_N)
 
     def c_send(t):
-        return remote(acc.at[other, tile(t)], cx.at[:, tile(t)], 11, c_r.at[t], twin)
+        return remote(acc.at[other, tile(t)], cx.at[:, tile(t)], 2, c_r.at[t], twin)
 
     def forward(t):
         acc[:, tile(t)] = jnp.dot(held[...], w[:, tile(t)], preferred_element_type=f32)
@@ -334,10 +337,10 @@
     def q_send(h):
         return remote(
             qt.at[:, at(width + h * HEAD_DIM, HEAD_DIM, HEAD_DIM)], qx.at[:, at(h * HEAD_DIM, HEAD_DIM, HEAD_DIM)],
-            12, one_sem.at[6], pair,
-        )
-
-    q_all = remote(qx, qx, 12, one_sem.at[6], pair)
+            2, one_sem.at[6], pair,
+        )
+
+    q_all = remote(qx, qx, 2, one_sem.at[6], pair)
 
     def joined(t):
         c_send(t).wait_recv()
@@ -422,7 +425,7 @@
         ng[:, at(core * half + q * quarter, quarter, quarter)] = part[home, ks]
     for way in range(2):
         ref = held.at[pl.ds(0, 2 * rows), :]
-        remote(ref, ref, 3, ag_r.at[way, 20], up).wait_recv()
+        remote(ref, ref, 1, ag_r.at[way, 20], up).wait_recv()
     loads[4].wait()
     bias_send.wait_recv()
 
@@ -510,21 +513,13 @@
     def sent(ref, send):
         remote(ref, ref, send, one_sem.at[0], twin).wait_send()
 
-    sent(w_h.at[pl.ds(0, (chunks + 1) * WCHUNK), :], 0)
-    sent(w_h.at[pl.ds(0, (chunks - 1) * WCHUNK), :], 1)
-    sent(nx, 2)
-    moved = held.at[pl.ds(0, 7 * 2 * rows), :]
-    sent(moved, 3)
+    sent(w_h.at[pl.ds(0, 2 * chunks * WCHUNK + 3 * col), :], 0)
+    sent(part.at[pl.ds(0, (2 * 7 + 1) * rows + rows // 2), :], 1)
+    sent(acc.at[pl.ds(0, col + col // 4), :], 2)
+    sent(gtot, 3)
     bias_send.wait_send()
-    sent(w_h.at[pl.ds(0, 3 * col), :], 5)
-    sent(moved, 6)
-    swap.wait_send()
-    sent(gx, 8)
-    sent(grecv, 9)
-    sent(grecv, 10)
-    sent(cx, 11)
-    sent(qx, 12)
-    gy_send.wait_send()
+    sent(grecv, 5)
+    sent(grecv, 6)
     g3_send.wait_send()
 
 
@@ -601,7 +596,7 @@
             vm((1, depth), f32),
             vm((8, width), f32),
             dma((6,)),
-            dma((15,)),
+            dma((8,)),
             dma((9,)),
             dma((3,)),
             dma((chunks,)),

time: 89.6 us -> 89.6 us (level)
  no operation moved by 1% of the time
where the time goes in v8:
time: 89.6 us; the launch traced here: 89.5 us
  Pallas kernels  88.8 us (99%)
    pallas_call x1, Pallas kernels, shards(): pl.pallas_call(functools.partial(kernel, nz, ndp), out_shape=(vm((every,...  87.6 us

profile of v8, /device:TPU:1, one launch (start us, length us, event | category | flops | bytes accessed | tf_op | source)
XLA Modules:
  0.0 89.5 jit_solution(15448807023353309854)
XLA Ops:
  0.6 87.6 %shard_map.93 = (bf16[512,640]{1,0:T(8,128)(2,1)S(1)}, f32[32,8192]{1,0:T(8,128)S(1)}, bf16[32,8192]{1,0:T(8,128)(2,1)S(1)}, f32[1,8192]{1,0:T(1,128)S(1)}, f32[...) custom-call(bf16[32,8192]{1,0:T(8,128)(2,1)} %tok_h.1, f32[8192]{0:T(1024)} %gain_h.1, ...), custom_call_target="tpu_custom_call" | custom-call | flops 10737418240 | bytes 10485760 | tf_op jit(solution)/shard_map/pallas_call | solution.py:559
  88.2 1.3 %shard_map.94 = (bf16[512,640]{1,0:T(8,128)(2,1)}, f32[32,8192]{1,0:T(8,128)}, f32[8192]{0:T(1024)}, f32[640]{0:T(1024)}) custom-call(bf16[512,640]{1,0:T(8,128)(2,1)S(1)} %get-tuple-element.11.qkv, f32[32,8192]{1,0:T(8,128)S(1)} %get-tuple-element.12.ng, bf16[32,8192]{1,0:T(8,128)(2,1)S(1)} %get-tuple-element.13.tok, f32[1,8192]{1,0:T(1,128)S(1)} %get-tuple-element.14.gain, ...), custom_call_target="tpu_custom_call" | custom-call | tf_op jit(solution)/shard_map/pallas_call | solution.py:619

commit v9 on v8

--- a/solution.py
+++ b/solution.py
@@ -182,7 +182,7 @@
 
     low_pair = remote(lowx, low.at[mine, pair_cols], 0, low_r.at[0], pair)
     low_twin = remote(low.at[mine, own_cols], low.at[mine, own_cols], 0, low_r.at[1], twin)
-    low_fwd = remote(low.at[mine, pair_cols], low.at[mine, pair_cols], 0, low_r.at[2], twin)
+    low_fwd = remote(low.at[mine, pair_cols], low.at[mine, pair_cols], 0, low_r.at[1], twin)
     low_pair.start()
     low_twin.start()
     for a in (2, 4, 6):
@@ -217,7 +217,7 @@
         return remote(
             run.at[way, j, pl.ds(d * rows, rows), cols(k)],
             rfin.at[way, :, at(core * half + k * CHUNK, CHUNK, CHUNK)],
-            1, end_r.at[way, core, jnp.where(j < 3, 0, jnp.where(k < chunks - 2, 1, 2))], dict(along[way], dp=dp - core + d),
+            1, end_r.at[jnp.where(j < 3, 0, jnp.where(k < chunks - 2, 1, 2))], dict(along[way], dp=dp - core + d),
         )
 
     def hops(way, k):
@@ -292,10 +292,8 @@
 
     def ended(group):
         count = (chunks // 2, chunks // 2 - 1, 1)[group]
-        for way in range(2):
-            for side in range(2):
-                ref = rfin.at[way, :, pl.ds(0, count * CHUNK)]
-                remote(ref, ref, 1, end_r.at[way, side, group], up).wait_recv()
+        ref = rfin.at[0, :, pl.ds(0, 4 * count * CHUNK)]
+        remote(ref, ref, 1, end_r.at[group], up).wait_recv()
 
     def gain_share(k):
         full = at(core * half + k * CHUNK, CHUNK, CHUNK)
@@ -328,7 +326,7 @@
         return at(t * TILE_N, TILE_N, TILE_N)
 
     def c_send(t):
-        return remote(acc.at[other, tile(t)], cx.at[:, tile(t)], 2, c_r.at[t], twin)
+        return remote(acc.at[other, tile(t)], cx.at[:, tile(t)], 2, c_r.at[0], twin)
 
     def forward(t):
         acc[:, tile(t)] = jnp.dot(held[...], w[:, tile(t)], preferred_element_type=f32)
@@ -342,8 +340,9 @@
 
     q_all = remote(qx, qx, 2, one_sem.at[6], pair)
 
+    c_all = remote(cx, cx, 2, c_r.at[0], twin)
+
     def joined(t):
-        c_send(t).wait_recv()
         for i in range(TILE_N // HEAD_DIM):
             h = t * (TILE_N // HEAD_DIM) + i
             hs = at(h * HEAD_DIM, HEAD_DIM, HEAD_DIM)
@@ -397,8 +396,7 @@
         @pl.when(i == 9)
         def _():
             loads[5].wait()
-            low_twin.wait_recv()
-            low_fwd.wait_recv()
+            remote(grad, grad, 0, low_r.at[1], twin).wait_recv()
 
         k, due = 0, i == early[0]
         for m in range(1, len(early)):
@@ -441,7 +439,11 @@
         for way in range(2):
             rs_step(way, j, jnp.where(j < 3, q, 2 * q + way))
 
-        @pl.when((m >= 2) & (m < 7))
+        @pl.when(m == 7)
+        def _():
+            c_all.wait_recv()
+
+        @pl.when((m >= 7) & (m < 12))
         def _():
             joined(lax.rem(m, 5))
 
@@ -551,7 +553,6 @@
     half, col, nz = depth // 2, every // 2, n // 2
     slab = half // nz
     chunks = half // CHUNK
-    tiles = 2 * width // TILE_N
     dma = pltpu.SemaphoreType.DMA
     vm = pltpu.VMEM
     hbm = pl.BlockSpec(memory_space=pl.ANY)
@@ -598,13 +599,13 @@
             dma((6,)),
             dma((8,)),
             dma((9,)),
-            dma((3,)),
+            dma((2,)),
             dma((chunks,)),
             dma((chunks,)),
             dma((2, 21)),
-            dma((2, 2, 3)),
+            dma((3,)),
             dma((2, TURNED)),
-            dma((tiles,)),
+            dma((1,)),
         ],
         compiler_params=pltpu.CompilerParams(
             collective_id=0, has_side_effects=True, vmem_limit_bytes=60000000

time: 89.6 us -> 89.6 us (level)
  no operation moved by 1% of the time
where the time goes in v9:
time: 89.6 us; the launch traced here: 89.5 us
  Pallas kernels  88.9 us (99%)
    pallas_call x1, Pallas kernels, shards(): pl.pallas_call(functools.partial(kernel, nz, ndp), out_shape=(vm((every,...  87.7 us

profile of v9, /device:TPU:1, one launch (start us, length us, event | category | flops | bytes accessed | tf_op | source)
XLA Modules:
  0.0 89.5 jit_solution(4731383140133040170)
XLA Ops:
  0.6 87.7 %shard_map.93 = (bf16[512,640]{1,0:T(8,128)(2,1)S(1)}, f32[32,8192]{1,0:T(8,128)S(1)}, bf16[32,8192]{1,0:T(8,128)(2,1)S(1)}, f32[1,8192]{1,0:T(1,128)S(1)}, f32[...) custom-call(bf16[32,8192]{1,0:T(8,128)(2,1)} %tok_h.1, f32[8192]{0:T(1024)} %gain_h.1, ...), custom_call_target="tpu_custom_call" | custom-call | flops 10737418240 | bytes 10485760 | tf_op jit(solution)/shard_map/pallas_call | solution.py:560
  88.3 1.3 %shard_map.94 = (bf16[512,640]{1,0:T(8,128)(2,1)}, f32[32,8192]{1,0:T(8,128)}, f32[8192]{0:T(1024)}, f32[640]{0:T(1024)}) custom-call(bf16[512,640]{1,0:T(8,128)(2,1)S(1)} %get-tuple-element.11.qkv, f32[32,8192]{1,0:T(8,128)S(1)} %get-tuple-element.12.ng, bf16[32,8192]{1,0:T(8,128)(2,1)S(1)} %get-tuple-element.13.tok, f32[1,8192]{1,0:T(1,128)S(1)} %get-tuple-element.14.gain, ...), custom_call_target="tpu_custom_call" | custom-call | tf_op jit(solution)/shard_map/pallas_call | solution.py:620

commit v10 on v9

--- a/solution.py
+++ b/solution.py
@@ -526,19 +526,22 @@
 
 
 def finish(qkv, ng, tok, gain, factors, gg, bg, qkv_h, tg_h, gg_h, bg_h, tg, sem):
-    parts = sem.shape[0] - 3
-    piece = tok.shape[1] // parts
+    parts = (sem.shape[0] - 2) // 2
+    rows, depth = tok.shape
+    piece, lines = rows // parts, qkv.shape[0] // parts
     copies = [
-        pltpu.make_async_copy(src, dst, sem.at[i])
-        for i, (src, dst) in enumerate(((qkv, qkv_h), (gg.at[0], gg_h), (bg.at[0], bg_h)))
+        pltpu.make_async_copy(src, dst, sem.at[i]) for i, (src, dst) in enumerate(((gg.at[0], gg_h), (bg.at[0], bg_h)))
     ]
+    for q in range(parts):
+        rs = slice(q * lines, (q + 1) * lines)
+        copies.append(pltpu.make_async_copy(qkv.at[rs], qkv_h.at[rs], sem.at[2 + q]))
     for c in copies:
         c.start()
-    scale, weight = factors[0, :, :1], factors[1, :, :1]
     for q in range(parts):
-        ks = slice(q * piece, (q + 1) * piece)
-        tg[:, ks] = scale * gain[:, ks] * ng[:, ks] - tok[:, ks].astype(jnp.float32) * weight
-        c = pltpu.make_async_copy(tg.at[:, ks], tg_h.at[:, ks], sem.at[3 + q])
+        rs = slice(q * piece, (q + 1) * piece)
+        scale, weight = factors[0, rs, :1], factors[1, rs, :1]
+        tg[rs] = scale * gain[...] * ng[rs] - tok[rs].astype(jnp.float32) * weight
+        c = pltpu.make_async_copy(tg.at[rs], tg_h.at[rs], sem.at[2 + parts + q])
         c.start()
         copies.append(c)
     for c in copies:
@@ -627,7 +630,7 @@
         ),
         in_specs=[vmem] * 7,
         out_specs=[hbm] * 4,
-        scratch_shapes=[vm((rows, depth), f32), dma((7,))],
+        scratch_shapes=[vm((rows, depth), f32), dma((2 + 2 * 4,))],
         compiler_params=pltpu.CompilerParams(vmem_limit_bytes=1 << 21),
     )(*results)
 

time: 89.6 us -> 89.7 us (level)
  no operation moved by 1% of the time
where the time goes in v10:
time: 89.7 us; the launch traced here: 89.6 us
  Pallas kernels  88.9 us (99%)
    pallas_call x1, Pallas kernels, shards(): pl.pallas_call(functools.partial(kernel, nz, ndp), out_shape=(vm((every,...  87.7 us

profile of v10, /device:TPU:1, one launch (start us, length us, event | category | flops | bytes accessed | tf_op | source)
XLA Modules:
  0.0 89.6 jit_solution(3131448989560603997)
XLA Ops:
  0.6 87.7 %shard_map.93 = (bf16[512,640]{1,0:T(8,128)(2,1)S(1)}, f32[32,8192]{1,0:T(8,128)S(1)}, bf16[32,8192]{1,0:T(8,128)(2,1)S(1)}, f32[1,8192]{1,0:T(1,128)S(1)}, f32[...) custom-call(bf16[32,8192]{1,0:T(8,128)(2,1)} %tok_h.1, f32[8192]{0:T(1024)} %gain_h.1, ...), custom_call_target="tpu_custom_call" | custom-call | flops 10737418240 | bytes 10485760 | tf_op jit(solution)/shard_map/pallas_call | solution.py:563
  88.3 1.3 %shard_map.94 = (bf16[512,640]{1,0:T(8,128)(2,1)}, f32[32,8192]{1,0:T(8,128)}, f32[8192]{0:T(1024)}, f32[640]{0:T(1024)}) custom-call(bf16[512,640]{1,0:T(8,128)(2,1)S(1)} %get-tuple-element.11.qkv, f32[32,8192]{1,0:T(8,128)S(1)} %get-tuple-element.12.ng, bf16[32,8192]{1,0:T(8,128)(2,1)S(1)} %get-tuple-element.13.tok, f32[1,8192]{1,0:T(1,128)S(1)} %get-tuple-element.14.gain, ...), custom_call_target="tpu_custom_call" | custom-call | tf_op jit(solution)/shard_map/pallas_call | solution.py:623
